TPU v7x, 128 devices: a whole 4x4x4 slice. The times are simulated.
128 devices in a mesh: dp: 8 (over z_hi, x), section: 4 (over y), tensor: 4 (over z_lo, core).
Axes of the slice: x: 4, y: 4, z: 4 (z_hi: 2, z_lo: 2; z = z_hi * 2 + z_lo), core: 2. Of those that a mesh axis runs over, the one named last changes fastest.
Arguments:
- failed_section: int32 [8], P('dp'), may hold values from 0 to 999
- token_ids: int32 [8, 2048], P('dp'), may hold values from 0 to 100001, as said below
- section_outputs: bfloat16 [8, 4, 2048, 2048], P('dp', 'section', None, 'tensor'), may hold values from -11 to 11
- w_query: float32 [4, 2048, 1024], P('section', 'dp', 'tensor'), may hold values from -1 to 1
- w_key: float32 [4, 2048, 1024], P('section', 'dp', 'tensor'), may hold values from -2 to 2
- w_value: float32 [4, 2048, 1024], P('section', 'dp', 'tensor'), may hold values from -0.125 to 0.125
- w_out: float32 [4, 2048, 1024], P('section', 'dp', 'tensor'), may hold values from -0.75 to 0.75
- m_value: float32 [4, 2048, 1024], P('section', 'dp', 'tensor'), may hold values from -3 to 3
- v_value: float32 [4, 2048, 1024], P('section', 'dp', 'tensor'), may hold values from 0.001 to 1
- m_out: float32 [4, 2048, 1024], P('section', 'dp', 'tensor'), may hold values from -3 to 3
- v_out: float32 [4, 2048, 1024], P('section', 'dp', 'tensor'), may hold values from 0.001 to 1
Outputs:
- restored_query: float32 [8, 4, 2048, 1024], P('dp', 'section', None, 'tensor')
- restored_key: float32 [8, 4, 2048, 1024], P('dp', 'section', None, 'tensor')
- restored_value: float32 [8, 4, 2048, 1024], P('dp', 'section', None, 'tensor')
- restored_out: float32 [8, 4, 2048, 1024], P('dp', 'section', None, 'tensor')
- restored_m_value: float32 [8, 4, 2048, 1024], P('dp', 'section', None, 'tensor')
- restored_v_value: float32 [8, 4, 2048, 1024], P('dp', 'section', None, 'tensor')
- restored_m_out: float32 [8, 4, 2048, 1024], P('dp', 'section', None, 'tensor')
- restored_v_out: float32 [8, 4, 2048, 1024], P('dp', 'section', None, 'tensor')
- attn_update: bfloat16 [8, 4, 2048, 2048], P('dp', 'section', None, 'tensor')
Inputs may be any that keep to these rules, and one draw needn't show every extreme that they name: `token_ids`: token ids of each replica's micro-batch; the id 100001 ends a document, the others are ordinary tokens below 100000.
All inputs are finite; a program needn't handle non-finite values.
Results may differ from a plain program's by a relative error of at most 0.0087.
Values may be sent and summed in bfloat16 or wider, within the bound.
A program may use at most 128 MiB of HBM per device.

v0:
```python
import math

import jax
import jax.numpy as jnp
from jax import lax
from jax.sharding import PartitionSpec as P

HD = 128


end_token = 100001
mask_fill = -1e30


def sent_together(arrays, axis, dim, along):
    ends, at = ([], 0)
    for a in arrays[:-1]:
        at += a.shape[along]
        ends.append(at)
    both = jnp.concatenate(arrays, axis=along)
    return tuple(jnp.split(lax.all_gather(both, axis, axis=dim, tiled=True), ends, axis=along))


def passed_along(array, axis, by):
    count = lax.axis_size(axis)
    return lax.ppermute(array, axis, [(i, (i + by) % count) for i in range(count)])


def document_ids(token_row):
    doc_ends = (token_row == end_token).astype(jnp.int32)
    return jnp.cumsum(doc_ends) - doc_ends


def attend(queries, key_vals, value_vals, token_row):
    token_count = queries.shape[0]
    heads_local = queries.shape[1] // HD
    block_rows = min(512, token_count)
    document = document_ids(token_row)
    positions = jnp.arange(token_count, dtype=jnp.int32)
    key_heads = key_vals.reshape(token_count, heads_local, HD)
    value_heads = value_vals.reshape(token_count, heads_local, HD)

    def one_block(block_index):
        first_row = block_index * block_rows
        query_block = lax.dynamic_slice_in_dim(queries, first_row, block_rows, 0).reshape(
            block_rows, heads_local, HD
        )
        scores = jnp.einsum(
            "qhd,khd->hqk", query_block, key_heads, preferred_element_type=jnp.float32
        ) * (1.0 / math.sqrt(HD))
        query_pos = lax.dynamic_slice_in_dim(positions, first_row, block_rows, 0)
        query_doc = lax.dynamic_slice_in_dim(document, first_row, block_rows, 0)
        allowed = (positions[None, :] <= query_pos[:, None]) & (
            document[None, :] == query_doc[:, None]
        )
        scores = jnp.where(allowed[None], scores, mask_fill)
        highest = jnp.max(scores, axis=2, keepdims=True)
        weights = jnp.exp(scores - highest)
        probs = (weights / jnp.sum(weights, axis=2, keepdims=True)).astype(jnp.bfloat16)
        context = jnp.einsum(
            "hqk,khd->qhd", probs, value_heads, preferred_element_type=jnp.float32
        ).astype(jnp.bfloat16)
        return context.reshape(block_rows, heads_local * HD)

    blocks = lax.map(one_block, jnp.arange(token_count // block_rows, dtype=jnp.int32))
    return blocks.reshape(token_count, heads_local * HD)


def shards(
    failed_section,
    token_ids,
    section_outputs,
    w_query,
    w_key,
    w_value,
    w_out,
    m_value,
    v_value,
    m_out,
    v_out,
):
    section_failed = jnp.remainder(failed_section[0], lax.axis_size("section"))
    replacing = lax.axis_index("section") == section_failed
    masters = tuple(
        (
            part.astype(jnp.float32)
            for part in sent_together(
                (
                    w_query.astype(jnp.bfloat16),
                    w_key.astype(jnp.bfloat16),
                    w_value.astype(jnp.bfloat16),
                    w_out.astype(jnp.bfloat16),
                ),
                "dp",
                1,
                0,
            )
        )
    )
    query_bf = masters[0][0].astype(jnp.bfloat16)
    key_bf = masters[1][0].astype(jnp.bfloat16)
    value_bf = masters[2][0].astype(jnp.bfloat16)
    out_bf = masters[3][0].astype(jnp.bfloat16)
    inner_local = query_bf.shape[1]
    w_joined = jnp.concatenate([query_bf, key_bf, value_bf], axis=1)
    incoming = passed_along(section_outputs, "section", 1)
    projected = jnp.dot(
        lax.all_gather(incoming, "tensor", axis=3, tiled=True)[0, 0],
        w_joined,
        preferred_element_type=jnp.float32,
    )
    queries = projected[:, :inner_local].astype(jnp.bfloat16)
    key_vals = projected[:, inner_local : 2 * inner_local].astype(jnp.bfloat16)
    value_vals = projected[:, 2 * inner_local :].astype(jnp.bfloat16)
    context = attend(queries, key_vals, value_vals, token_ids[0])
    context_whole = lax.all_gather(context, "tensor", axis=1, tiled=True)
    out_slice = lax.all_to_all(out_bf, "tensor", split_axis=0, concat_axis=1, tiled=True)
    update = lax.dot_general(
        context_whole, out_slice, (((1,), (1,)), ((), ())), preferred_element_type=jnp.float32
    ).astype(jnp.bfloat16)
    moments = tuple(
        (
            part.astype(jnp.float32)
            for part in sent_together(
                (
                    m_value.astype(jnp.bfloat16),
                    v_value.astype(jnp.bfloat16),
                    m_out.astype(jnp.bfloat16),
                    v_out.astype(jnp.bfloat16),
                ),
                "dp",
                1,
                0,
            )
        )
    )

    def placed(gathered):
        return jnp.where(replacing, gathered[None], jnp.zeros_like(gathered[None]))

    update_block = jnp.where(
        replacing, update[None, None], jnp.zeros((1, 1) + update.shape, jnp.bfloat16)
    )
    return (
        placed(masters[0]),
        placed(masters[1]),
        placed(masters[2]),
        placed(masters[3]),
        placed(moments[0]),
        placed(moments[1]),
        placed(moments[2]),
        placed(moments[3]),
        update_block,
    )


def solution(mesh):
    return jax.shard_map(
        shards,
        mesh=mesh,
        in_specs=(
            P("dp"),
            P("dp", None),
            P("dp", "section", None, "tensor"),
            P("section", "dp", "tensor"),
            P("section", "dp", "tensor"),
            P("section", "dp", "tensor"),
            P("section", "dp", "tensor"),
            P("section", "dp", "tensor"),
            P("section", "dp", "tensor"),
            P("section", "dp", "tensor"),
            P("section", "dp", "tensor"),
        ),
        out_specs=(
            P("dp", "section", None, "tensor"),
            P("dp", "section", None, "tensor"),
            P("dp", "section", None, "tensor"),
            P("dp", "section", None, "tensor"),
            P("dp", "section", None, "tensor"),
            P("dp", "section", None, "tensor"),
            P("dp", "section", None, "tensor"),
            P("dp", "section", None, "tensor"),
            P("dp", "section", None, "tensor"),
        ),
        check_vma=False,
    )
```

profile of v0, /device:TPU:1, one launch (start us, length us, event | category | flops | bytes accessed | tf_op | source)
XLA Modules:
  0.0 302.3 jit_solution(5347417715151155394)
XLA Ops:
  7.2 0.0 all-gather.5.cloned.1.call-start
  7.3 1.0 convert_element_type.92
  8.3 1.0 convert_element_type.93
  9.3 1.0 convert_element_type.94
  10.2 1.0 convert_element_type.95
  11.2 0.9 pad_maximum_fusion
  12.1 0.0 all-gather.5.cloned.1.call-update
  12.1 0.0 all-gather.9.cloned.1.call-start
  12.2 2.2 collective-permute-start
  14.3 47.0 %collective-permute-done = bf16[1,1,2048,512]{3,2,1,0:T(8,128)(2,1)S(1)} collective-permute-done((bf16[1,1,2048,512]{3,2,1,0:T(8,128)(2,1)}, bf16[1,1,2048,512]{3,2,1,0:T(8,128)(2,1)S(1)}, u32[]{:S(2)}, u32[]{:S(2)}) %collective-permute-start) | collective-permute-done | bytes 2097184 | tf_op jit(solution)/shard_map/ppermute | solution.py:26
  61.3 1.3 copy-done
  62.7 0.0 all-gather.7.cloned.1.call-start
  62.9 0.9 pad_maximum_fusion.1
  63.7 0.0 all-gather.11.cloned.1.call-start
  63.8 0.3 reduce-window.9
  64.1 0.1 slice.24
  64.2 0.1 slice_reduce_fusion
  64.3 0.1 bitcast_subtract_fusion
  64.4 21.9 %all-gather.5.cloned.1.call-done = bf16[4,2048,256]{2,1,0:T(8,128)(2,1)} async-done(((bf16[4,256,256]{2,1,0:T(8,128)(2,1)}), bf16[4,2048,256]{2,1,0:T(8,128)(2,1)}) %all-gather.5.cloned.1.call-update) | async-done | bytes 4194320 | tf_op jit(solution)/shard_map/all_gather | solution.py:21
  86.3 3.4 %fusion.30 = (bf16[1,2048,256]{2,1,0:T(8,128)(2,1)}, bf16[2048,256]{1,0:T(8,128)(2,1)S(1)}, bf16[2048,256]{1,0:T(8,128)(2,1)S(1)}, bf16[2048,256]{1,0:T(8,128)(2,1)S(1)}) fusion(bf16[4,2048,256]{2,1,0:T(8,128)(2,1)} %all-gather.5.cloned.1.call-done), kind=kLoop, calls=%fused_computation.46 | loop fusion | bytes 8388608 | tf_op jit(solution)/shard_map/split | solution.py:21
  89.7 79.1 %all-gather.9.cloned.1.call-done = bf16[1,1,2048,2048]{3,2,1,0:T(8,128)(2,1)} async-done(((bf16[1,1,2048,512]{3,2,1,0:T(8,128)(2,1)}), bf16[1,1,2048,2048]{3,2,1,0:T(8,128)(2,1)}) %all-gather.9.cloned.1.call-update) | async-done | bytes 8388624 | tf_op jit(solution)/shard_map/all_gather | solution.py:108
  168.8 9.1 %fusion.21 = bf16[2048,768]{0,1:T(8,128)(2,1)S(1)} fusion(bf16[1,1,2048,2048]{3,2,1,0:T(8,128)(2,1)} %all-gather.9.cloned.1.call-done, bf16[2048,256]{1,0:T(8,128)(2,1)S(1)} %get-tuple-element.120, bf16[2048,256]{1,0:T(8,128)(2,1)S(1)} %get-tuple-element.119, bf16[2048,256]{1,0:T(8,128)(2,1)S(1)} %get-tuple-element.118), kind=kOutput, calls=%fused_computation.24 | convolution fusion | flops 6453460992 | bytes 14680064 | tf_op jit(solution)/shard_map/dot_general | solution.py:107
  178.0 1.2 fusion.31
  179.2 0.7 copy.26
  179.9 54.7 %while.11 = (s32[]{:T(128)}, bf16[4,512,256]{2,1,0:T(8,128)(2,1)}, s32[2048]{0:T(1024)S(1)}, s32[4]{0:T(128)S(1)}, s32[2048]{0:T(1024)S(1)}, /*index=5*/bf16[204...) while((s32[]{:T(128)}, bf16[4,512,256]{2,1,0:T(8,128)(2,1)}, ...), condition=%wide.region_5.6_spmd.clone, body=%wide.region_2.5_spmd.clone.sunk | while | flops 1089603584 | bytes 23106236 | solution.py:65
  179.9 0.6 dynamic_slice.23
  181.2 0.1 dynamic_slice.24
  181.3 0.1 dynamic_slice.25
  181.3 0.9 compare_and_fusion.2
  182.3 5.2 %fusion.47 = (f32[2,512]{1,0:T(2,128)S(1)}, f32[2,512,2048]{2,1,0:T(8,128)}) fusion(pred[512,2048]{1,0:T(8,128)(4,1)S(1)} %compare_and_fusion.2, bf16[512,2,128]{0,2,1:T(8,128)(2,1)S(1)} %bitcast.71, bf16[2048,2,128]{2,0,1:T(8,128)(2,1)S(1)} %get-tuple-element.215), kind=kOutput, calls=%fused_computation.45.clone.1 | convolution fusion | flops 545261568 | bytes 10752000 | tf_op jit(solution)/shard_map/while/body/eval_jaxpr/sub | solution.py:58
  187.5 5.2 %fusion.48 = bf16[2,512,128]{1,2,0:T(8,128)(2,1)S(1)} fusion(bf16[2048,2,128]{0,2,1:T(8,128)(2,1)} %get-tuple-element.216, f32[2,512,2048]{2,1,0:T(8,128)} %get-tuple-element.183, f32[2,512]{1,0:T(2,128)S(1)} %get-tuple-element.184), kind=kOutput, calls=%fused_computation.10.clone.1 | convolution fusion | flops 541196288 | bytes 9703424 | tf_op jit(solution)/shard_map/while/body/eval_jaxpr/hqk,khd->qhd/dot_general | solution.py:60
  192.7 0.1 copy.33
  192.9 0.7 constant_dynamic-update-slice_fusion.2
  193.6 0.6 dynamic_slice.23
  194.9 0.1 dynamic_slice.24
  194.9 0.1 dynamic_slice.25
  195.0 0.9 compare_and_fusion.2
  196.0 5.2 %fusion.47 = (f32[2,512]{1,0:T(2,128)S(1)}, f32[2,512,2048]{2,1,0:T(8,128)}) fusion(pred[512,2048]{1,0:T(8,128)(4,1)S(1)} %compare_and_fusion.2, bf16[512,2,128]{0,2,1:T(8,128)(2,1)S(1)} %bitcast.71, bf16[2048,2,128]{2,0,1:T(8,128)(2,1)S(1)} %get-tuple-element.215), kind=kOutput, calls=%fused_computation.45.clone.1 | convolution fusion | flops 545261568 | bytes 10752000 | tf_op jit(solution)/shard_map/while/body/eval_jaxpr/sub | solution.py:58
  201.2 5.2 %fusion.48 = bf16[2,512,128]{1,2,0:T(8,128)(2,1)S(1)} fusion(bf16[2048,2,128]{0,2,1:T(8,128)(2,1)} %get-tuple-element.216, f32[2,512,2048]{2,1,0:T(8,128)} %get-tuple-element.183, f32[2,512]{1,0:T(2,128)S(1)} %get-tuple-element.184), kind=kOutput, calls=%fused_computation.10.clone.1 | convolution fusion | flops 541196288 | bytes 9703424 | tf_op jit(solution)/shard_map/while/body/eval_jaxpr/hqk,khd->qhd/dot_general | solution.py:60
  206.4 0.1 copy.33
  206.5 0.7 constant_dynamic-update-slice_fusion.2
  207.3 0.6 dynamic_slice.23
  208.5 0.1 dynamic_slice.24
  208.6 0.1 dynamic_slice.25
  208.7 0.9 compare_and_fusion.2
  209.6 5.2 %fusion.47 = (f32[2,512]{1,0:T(2,128)S(1)}, f32[2,512,2048]{2,1,0:T(8,128)}) fusion(pred[512,2048]{1,0:T(8,128)(4,1)S(1)} %compare_and_fusion.2, bf16[512,2,128]{0,2,1:T(8,128)(2,1)S(1)} %bitcast.71, bf16[2048,2,128]{2,0,1:T(8,128)(2,1)S(1)} %get-tuple-element.215), kind=kOutput, calls=%fused_computation.45.clone.1 | convolution fusion | flops 545261568 | bytes 10752000 | tf_op jit(solution)/shard_map/while/body/eval_jaxpr/sub | solution.py:58
  214.8 5.3 %fusion.48 = bf16[2,512,128]{1,2,0:T(8,128)(2,1)S(1)} fusion(bf16[2048,2,128]{0,2,1:T(8,128)(2,1)} %get-tuple-element.216, f32[2,512,2048]{2,1,0:T(8,128)} %get-tuple-element.183, f32[2,512]{1,0:T(2,128)S(1)} %get-tuple-element.184), kind=kOutput, calls=%fused_computation.10.clone.1 | convolution fusion | flops 541196288 | bytes 9703424 | tf_op jit(solution)/shard_map/while/body/eval_jaxpr/hqk,khd->qhd/dot_general | solution.py:60
  220.1 0.1 copy.33
  220.2 0.7 constant_dynamic-update-slice_fusion.2
  221.0 0.6 dynamic_slice.23
  222.2 0.1 dynamic_slice.24
  222.3 0.1 dynamic_slice.25
  222.4 0.9 compare_and_fusion.2
  223.3 5.2 %fusion.47 = (f32[2,512]{1,0:T(2,128)S(1)}, f32[2,512,2048]{2,1,0:T(8,128)}) fusion(pred[512,2048]{1,0:T(8,128)(4,1)S(1)} %compare_and_fusion.2, bf16[512,2,128]{0,2,1:T(8,128)(2,1)S(1)} %bitcast.71, bf16[2048,2,128]{2,0,1:T(8,128)(2,1)S(1)} %get-tuple-element.215), kind=kOutput, calls=%fused_computation.45.clone.1 | convolution fusion | flops 545261568 | bytes 10752000 | tf_op jit(solution)/shard_map/while/body/eval_jaxpr/sub | solution.py:58
  228.5 5.2 %fusion.48 = bf16[2,512,128]{1,2,0:T(8,128)(2,1)S(1)} fusion(bf16[2048,2,128]{0,2,1:T(8,128)(2,1)} %get-tuple-element.216, f32[2,512,2048]{2,1,0:T(8,128)} %get-tuple-element.183, f32[2,512]{1,0:T(2,128)S(1)} %get-tuple-element.184), kind=kOutput, calls=%fused_computation.10.clone.1 | convolution fusion | flops 541196288 | bytes 9703424 | tf_op jit(solution)/shard_map/while/body/eval_jaxpr/hqk,khd->qhd/dot_general | solution.py:60
  233.7 0.1 copy.33
  233.9 0.7 constant_dynamic-update-slice_fusion.2
  235.3 3.7 %all-to-all-start = ((bf16[4,512,256]{2,1,0:T(8,128)(2,1)}), bf16[4,512,256]{2,1,0:T(8,128)(2,1)S(1)}, u32[]{:S(2)}, u32[]{:S(2)}) async-start(bf16[4,512,256]{2,1,0:T(8,128)(2,1)} %bitcast.20), calls=%async_computation | async-start | bytes 2097152 | tf_op jit(solution)/shard_map/all_to_all | solution.py:117
  239.0 5.7 %select_bitcast_fusion.4 = (f32[1,1,2048,256]{3,2,1,0:T(8,128)}, f32[1,1,2048,256]{3,2,1,0:T(8,128)}, f32[1,1,2048,256]{3,2,1,0:T(8,128)}, f32[1,1,2048,256]{3,2,1,0:T(8,128)}) fusion(pred[]{:T(512)S(6)} %eq.31, bf16[4,2048,256]{2,1,0:T(8,128)(2,1)} %all-gather.5.cloned.1.call-done), kind=kLoop, calls=%fused_computation.32 | loop fusion | flops 4194304 | bytes 12582913 | tf_op jit(solution)/shard_map/jit(_where)/select_n | solution.py:139
  244.7 5.7 %select_bitcast_fusion = (f32[1,1,2048,256]{3,2,1,0:T(8,128)}, f32[1,1,2048,256]{3,2,1,0:T(8,128)}, f32[1,1,2048,256]{3,2,1,0:T(8,128)}, f32[1,1,2048,256]{3,2,1,0:T(8,128)}) fusion(bf16[4,2048,256]{2,1,0:T(8,128)(2,1)} %all-gather.7.cloned.1.call-done, pred[]{:T(512)S(6)} %eq.31), kind=kLoop, calls=%fused_computation.28 | loop fusion | flops 4194304 | bytes 12582913 | tf_op jit(solution)/shard_map/jit(_where)/select_n | solution.py:139
  250.3 0.8 all-to-all-done
  251.1 0.5 copy.28
  251.6 38.3 %all-gather.11.cloned.1.call-done = bf16[2048,1024]{1,0:T(8,128)(2,1)} async-done(((bf16[2048,256]{1,0:T(8,128)(2,1)}), bf16[2048,1024]{1,0:T(8,128)(2,1)}) %all-gather.11.cloned.1.call-update) | async-done | bytes 4194320 | tf_op jit(solution)/shard_map/all_gather | solution.py:116
  290.0 5.8 %fusion.27 = bf16[1,1,2048,512]{3,2,1,0:T(8,128)(2,1)} fusion(bf16[2048,1024]{1,0:T(8,128)(2,1)} %all-gather.11.cloned.1.call-done, bf16[512,1024]{0,1:T(8,128)(2,1)S(1)} %bitcast.76, pred[]{:T(512)S(6)} %eq.31), kind=kOutput, calls=%fused_computation.27 | convolution fusion | flops 2149580800 | bytes 7340033 | tf_op jit(solution)/shard_map/dot_general | solution.py:118
  (28 shorter events, 0.3 us)
Async XLA Ops:
  7.2 55.5 %copy-start.1 = (f32[1,256,256]{2,1,0:T(8,128)S(1)}, f32[1,256,256]{2,1,0:T(8,128)}, u32[]{:S(2)}) copy-start(f32[1,256,256]{2,1,0:T(8,128)} %param.20) | copy-start | bytes 786436
  7.2 55.6 %copy-start.2 = (f32[1,256,256]{2,1,0:T(8,128)S(1)}, f32[1,256,256]{2,1,0:T(8,128)}, u32[]{:S(2)}) copy-start(f32[1,256,256]{2,1,0:T(8,128)} %param.21) | copy-start | bytes 786436
  7.2 55.6 %copy-start.3 = (f32[1,256,256]{2,1,0:T(8,128)S(1)}, f32[1,256,256]{2,1,0:T(8,128)}, u32[]{:S(2)}) copy-start(f32[1,256,256]{2,1,0:T(8,128)} %param.22) | copy-start | bytes 786436
  7.2 55.6 %copy-start.4 = (f32[1,256,256]{2,1,0:T(8,128)S(1)}, f32[1,256,256]{2,1,0:T(8,128)}, u32[]{:S(2)}) copy-start(f32[1,256,256]{2,1,0:T(8,128)} %param.23) | copy-start | bytes 786436
  7.2 79.1 %all-gather.5.cloned.1.call-start = ((), (), s32[]{:S(2)}) async-start(), calls=%async_computation.1 | async-start | bytes 4718592 | tf_op jit(solution)/shard_map/all_gather | solution.py:21
  12.1 51.7 %copy-start.5 = (s32[1,2048]{1,0:T(1,128)S(1)}, s32[1,2048]{1,0:T(1,128)}, u32[]{:S(2)}) copy-start(s32[1,2048]{1,0:T(1,128)} %param.14) | copy-start | bytes 24580
  12.1 156.7 %all-gather.9.cloned.1.call-start = ((), (), s32[]{:S(2)}) async-start(), calls=%async_computation.3 | async-start | bytes 10485760 | tf_op jit(solution)/shard_map/all_gather | solution.py:108
  12.2 49.2 %collective-permute-start = (bf16[1,1,2048,512]{3,2,1,0:T(8,128)(2,1)}, bf16[1,1,2048,512]{3,2,1,0:T(8,128)(2,1)S(1)}, u32[]{:S(2)}, u32[]{:S(2)}) collective-permute-start(bf16[1,1,2048,512]{3,2,1,0:T(8,128)(2,1)} %param.15), channel_id=1, source_target_pairs={{0,4},{4,8},{8,12},{12,0},{1,5},{5,9},{9,13},{13,1},{2,6},{6,10},{... | collective-permute-start | bytes 6291464 | tf_op jit(solution)/shard_map/ppermute | solution.py:26
  61.3 1.3 copy-start
  62.7 182.0 %all-gather.7.cloned.1.call-start = ((), (), s32[]{:S(2)}) async-start(), calls=%async_computation.2 | async-start | bytes 4718592 | tf_op jit(solution)/shard_map/all_gather | solution.py:21
  63.7 226.2 %all-gather.11.cloned.1.call-start = ((), (), s32[]{:S(2)}) async-start(), calls=%async_computation.4 | async-start | bytes 5242880 | tf_op jit(solution)/shard_map/all_gather | solution.py:116
  235.3 15.8 %all-to-all-start = ((bf16[4,512,256]{2,1,0:T(8,128)(2,1)}), bf16[4,512,256]{2,1,0:T(8,128)(2,1)S(1)}, u32[]{:S(2)}, u32[]{:S(2)}) async-start(bf16[4,512,256]{2,1,0:T(8,128)(2,1)} %bitcast.20), calls=%async_computation | async-start | bytes 2097152 | tf_op jit(solution)/shard_map/all_to_all | solution.py:117
Sparse Core Ops, SparseCore 0:
  12.2 74.0 all-gather.4
  88.5 80.2 all-gather.8
  171.8 71.3 all-gather.6
  244.7 45.2 all-gather.10
where the time goes:
time: 303 us; the launch traced here: 302 us
  waiting for transfers between devices  187 us (62%)
  matrix products  56.7 us (19%)
  other arithmetic  21.1 us (7%)
  between operations  14.6 us (5%)
  local copies, waits for them, and re-layouts  13.9 us (5%)
  starting transfers between devices  6.04 us (2%)
    all_gather x1, waiting for transfers between devices, shards(): lax.all_gather(incoming, 'tensor', axis=3, tiled=True)[0, 0]  79.1 us
    ppermute x1, waiting for transfers between devices, passed_along(): lax.ppermute(array, axis, [(i, (i + by) % count) for i in range(count)])  47 us
    all_gather x1, waiting for transfers between devices, shards(): context_whole = lax.all_gather(context, 'tensor', axis=1, tiled=True)  38.3 us
    all_gather x2, waiting for transfers between devices, sent_together(): lax.all_gather(both, axis, axis=dim, tiled=True)  21.9 us
    dot_general x4, matrix products, one_block(): jnp.einsum('hqk,khd->qhd', probs, value_heads, preferred_element_type=jnp...  20.9 us
    sub x4, matrix products, one_block(): weights = jnp.exp(scores - highest)  20.8 us
    select_n x2, other arithmetic, placed(): return jnp.where(replacing, gathered[None], jnp.zeros_like(gathered[None]))  11.3 us
    dot_general x1, matrix products, shards(): jnp.dot(lax.all_gather(incoming, 'tensor', axis=3, tiled=True)[0, 0], w_j...  9.14 us
  transfers between devices with their start and end apart: 6, of which 5 were waited for; matrix products, arithmetic and copies ran while one was open for 26% of the time, Pallas kernels for 0%

commit v1 on v0

v1 whole, which is shorter than its diff:
```python
import math

import jax
import jax.numpy as jnp
from jax import lax
from jax.experimental import pallas as pl
from jax.experimental.pallas import tpu as pltpu
from jax.sharding import PartitionSpec as P

MESH = pl.DeviceIdType.MESH
HD = 128
END_TOKEN = 100001
FILL = -1e30
SCALE = 1.0 / math.sqrt(HD)

ROWS = 2048
CHUNK = 256
STEPS = ROWS // CHUNK
SHARD = 256
FEATS = 512
HALF = SHARD // 2

GROUPS = ((0, 3), (3, 1), (4, 1), (5, 1), (6, 1), (7, 1))
LOOP = 12


def produced(i):
    return jnp.clip(jnp.minimum(2 * (i - 4), i - 1), 0, STEPS)


def gather_attend(
    tok, x, wq, wk, wv, wo, mv, vv, mo, vo,
    full, ctx_full, wo_rows,
    own, xs, wb, qb, kb, vb, cb, ends, bounce,
    w_send, w_recv, x_send, x_recv, c_send, c_recv, o_send, o_recv, local_sem,
):
    r = lax.axis_index("dp")
    s = lax.axis_index("section")
    t = lax.axis_index("tensor")
    zh, xi = r // 4, r % 4
    right = zh * 4 + (xi + 1) % 4
    left = zh * 4 + (xi + 3) % 4
    twin = (r + 4) % 8
    down = (s + 1) % 4
    up = (s + 3) % 4
    core = (t // 2) * 2 + (t + 1) % 2
    pair = (t + 2) % 4
    cross = (core + 2) % 4

    for index, ref in enumerate((wq, wk, wv, wo, mv, vv, mo, vo)):
        own[index] = ref[...].astype(jnp.bfloat16)

    barrier = pltpu.get_barrier_semaphore()
    peers = (
        {"dp": right}, {"dp": left}, {"dp": twin}, {"section": down}, {"section": up},
        {"tensor": core}, {"tensor": pair}, {"tensor": cross},
    )
    for peer in peers:
        pl.semaphore_signal(barrier, inc=1, device_id=peer, device_id_type=MESH)
    pl.semaphore_wait(barrier, len(peers))

    def remote(src, dst, send, recv, to):
        return pltpu.make_async_remote_copy(
            src_ref=src, dst_ref=dst, send_sem=send, recv_sem=recv, device_id=to, device_id_type=MESH
        )

    def place(g, block, first=0, count=SHARD):
        start, n = GROUPS[g]
        return full.at[pl.ds(start, n), pl.ds(pl.multiple_of(block * SHARD + first, HALF), count), :]

    def w_copy(g, kind):
        start, n = GROUPS[g]
        mine = own.at[pl.ds(start, n)]
        sems = w_send.at[g, kind], w_recv.at[g, kind]
        if kind == 0:
            return remote(mine, place(g, r), *sems, {"dp": twin})
        if kind == 1:
            return remote(mine, place(g, r), *sems, {"dp": right})
        if kind == 2:
            return remote(mine, place(g, r), *sems, {"dp": left})
        if kind == 3:
            return remote(place(g, twin), place(g, twin), *sems, {"dp": right})
        if kind == 4:
            return remote(place(g, twin), place(g, twin), *sems, {"dp": left})
        source = (left, right, (left + 4) % 8, (right + 4) % 8)[kind - 5]
        to = right if kind in (5, 7) else left
        half = place(g, source, 0 if kind in (5, 7) else HALF, HALF)
        return remote(half, half, *sems, {"dp": to})

    def w_own(g):
        w_copy(g, 0).start()
        w_copy(g, 1).start()
        w_copy(g, 2).start()

    def w_twin(g):
        w_copy(g, 0).wait_recv()
        w_copy(g, 3).start()
        w_copy(g, 4).start()

    def w_on(g):
        for kind in (1, 2):
            w_copy(g, kind).wait_recv()
            w_copy(g, kind + 4).start()

    def w_twin_on(g):
        for kind in (3, 4):
            w_copy(g, kind).wait_recv()
            w_copy(g, kind + 4).start()

    def w_whole(g):
        for kind in (5, 6, 7, 8):
            w_copy(g, kind).wait_recv()

    def rows(c):
        return pl.ds(pl.multiple_of(c * CHUNK, CHUNK), CHUNK)

    def x_copy(c, kind):
        sems = x_send.at[kind, c], x_recv.at[kind, c]
        if kind == 0:
            return remote(x.at[rows(c), :], xs.at[t, rows(c), :], *sems, {"section": down})
        slot = pair if kind == 3 else t
        part = xs.at[slot, rows(c), :]
        return remote(part, part, *sems, {"tensor": pair if kind == 1 else core})

    def c_copy(c, kind):
        sems = c_send.at[kind, c], c_recv.at[kind, c]
        if kind == 2:
            part = ctx_full.at[pair, rows(c), :]
            return remote(part, part, *sems, {"tensor": core})
        return remote(cb.at[rows(c), :], ctx_full.at[t, rows(c), :], *sems, {"tensor": pair if kind == 0 else core})

    def o_copy(kind):
        to = (pair, core, cross)[kind]
        src = full.at[3, pl.ds(pl.multiple_of(to * FEATS, FEATS), FEATS), :]
        return remote(src, wo_rows.at[t], o_send.at[kind], o_recv.at[kind], {"tensor": to})

    w_own(0)
    lax.fori_loop(0, STEPS, lambda c, _: (x_copy(c, 0).start(), 0)[1], 0)
    keep = [
        pltpu.make_async_copy(own.at[pl.ds(n0, n)], place(g, r), local_sem.at[g])
        for g, (n0, n) in enumerate(GROUPS)
    ]
    for copy in keep:
        copy.start()
    where = lax.broadcasted_iota(jnp.int32, (1, ROWS), 1).astype(jnp.float32)
    ends[...] = jnp.where(tok[...] == END_TOKEN, where + 1.0, 0.0)

    def attend(c, _):
        for kind in (2, 3):
            x_copy(c, kind).wait_recv()
        for a, dst in enumerate((qb, kb, vb)):
            total = jnp.zeros((CHUNK, SHARD), jnp.float32)
            for part in range(4):
                total += jnp.dot(
                    xs[part, rows(c), :], wb[a, part * FEATS : (part + 1) * FEATS, :],
                    preferred_element_type=jnp.float32,
                )
            if a == 0:
                dst[...] = total.astype(jnp.bfloat16)
            else:
                dst[rows(c), :] = total.astype(jnp.bfloat16)
        row = (c * CHUNK + lax.broadcasted_iota(jnp.int32, (CHUNK, 1), 0)).astype(jnp.float32)
        first = jnp.max(jnp.where(where < row, ends[...], 0.0), axis=1, keepdims=True)

        def step(j, carry):
            col = (j * CHUNK + lax.broadcasted_iota(jnp.int32, (1, CHUNK), 1)).astype(jnp.float32)
            allowed = (col <= row) & (col >= first)
            new = []
            for h in range(2):
                highest, total, acc = carry[h]
                lanes = slice(h * HD, (h + 1) * HD)
                scores = lax.dot_general(
                    qb[:, lanes], kb[rows(j), lanes], (((1,), (1,)), ((), ())),
                    preferred_element_type=jnp.float32,
                ) * SCALE
                scores = jnp.where(allowed, scores, FILL)
                top = jnp.maximum(highest, jnp.max(scores, axis=1, keepdims=True))
                weights = jnp.exp(scores - top)
                shrink = jnp.exp(highest - top)
                total = total * shrink + jnp.sum(weights, axis=1, keepdims=True)
                acc = acc * shrink + jnp.dot(
                    weights.astype(jnp.bfloat16), vb[rows(j), lanes], preferred_element_type=jnp.float32
                )
                new.append((top, total, acc))
            return tuple(new)

        begin = (
            jnp.full((CHUNK, 1), FILL, jnp.float32),
            jnp.zeros((CHUNK, 1), jnp.float32),
            jnp.zeros((CHUNK, HD), jnp.float32),
        )
        done = lax.fori_loop(0, c + 1, step, (begin, begin))
        for h in range(2):
            _, total, acc = done[h]
            cb[rows(c), h * HD : (h + 1) * HD] = (acc / total).astype(jnp.bfloat16)
        return 0

    def send_context(c, _):
        c_copy(c, 0).start()
        c_copy(c, 1).start()
        pltpu.make_async_copy(cb.at[rows(c), :], ctx_full.at[t, rows(c), :], c_send.at[3, c]).start()
        return 0

    events = {step: [] for step in range(LOOP)}
    events[1] += [(w_twin, 0), (w_on, 0)]
    events[3] += [(w_twin_on, 0)]
    events[5] += [(w_whole, 0)]
    for g in range(1, 6):
        events[g] += [(w_own, g)]
        events[g + 2] += [(w_on, g)]
        events[g + 3] += [(w_twin, g)]
        events[g + 6] += [(w_twin_on, g)]

    def loop(i, _):
        @pl.when(i < STEPS)
        def _():
            x_copy(i, 0).wait_recv()
            x_copy(i, 1).start()
            x_copy(i, 2).start()

        for at, todo in events.items():
            if todo:
                @pl.when(i == at)
                def _(todo=todo, at=at):
                    for act, g in todo:
                        act(g)
                    if at == 5:
                        for copy in keep:
                            copy.wait()
                        load = pltpu.make_async_copy(full.at[pl.ds(0, 3)], wb, local_sem.at[6])
                        load.start()
                        load.wait()

        @pl.when((i >= 2) & (i < STEPS + 2))
        def _():
            x_copy(i - 2, 1).wait_recv()
            x_copy(i - 2, 3).start()

        lax.fori_loop(produced(i - 2), produced(i - 1), send_context, 0)
        lax.fori_loop(produced(i - 1), produced(i), attend, 0)
        return 0

    lax.fori_loop(0, LOOP, loop, 0)

    w_whole(1)
    for kind in range(3):
        o_copy(kind).start()
    mine = pl.ds(pl.multiple_of(t * FEATS, FEATS), FEATS)
    load = pltpu.make_async_copy(full.at[3, mine, :], bounce, local_sem.at[6])
    load.start()
    load.wait()
    store = pltpu.make_async_copy(bounce, wo_rows.at[t], local_sem.at[6])
    store.start()

    def forward_context(c, _):
        c_copy(c, 0).wait_recv()
        c_copy(c, 2).start()
        return 0

    lax.fori_loop(0, STEPS, forward_context, 0)
    for g in range(2, 6):
        w_whole(g)
    for kind in range(3):
        o_copy(kind).wait()
    store.wait()

    def finish(c, _):
        for kind in range(4):
            x_copy(c, kind).wait_send()
        c_copy(c, 0).wait_send()
        c_copy(c, 1).wait()
        c_copy(c, 2).wait()
        pltpu.make_async_copy(cb.at[rows(c), :], ctx_full.at[t, rows(c), :], c_send.at[3, c]).wait()
        return 0

    lax.fori_loop(0, STEPS, finish, 0)
    for g in range(6):
        for kind in range(9):
            w_copy(g, kind).wait_send()


def place_blocks(failed, full, ctx, wo_rows, *outs):
    replacing = lax.rem(failed[0], 4) == lax.axis_index("section")
    for a in range(8):
        outs[a][0, 0] = jnp.where(replacing, full[a].astype(jnp.float32), 0.0)
    total = jnp.zeros((CHUNK, FEATS), jnp.float32)
    for part in range(4):
        total += lax.dot_general(
            ctx[part], wo_rows[part], (((1,), (1,)), ((), ())), preferred_element_type=jnp.float32
        )
    outs[8][0, 0] = jnp.where(replacing, total, 0.0).astype(jnp.bfloat16)


def shards(failed_section, token_ids, section_outputs, *weights):
    bf16 = jnp.bfloat16
    vmem = pl.BlockSpec(memory_space=pltpu.VMEM)
    hbm = pl.BlockSpec(memory_space=pl.ANY)
    dma = pltpu.SemaphoreType.DMA
    full, ctx, wo_rows = pl.pallas_call(
        gather_attend,
        out_shape=(
            jax.ShapeDtypeStruct((8, ROWS, SHARD), bf16),
            jax.ShapeDtypeStruct((4, ROWS, SHARD), bf16),
            jax.ShapeDtypeStruct((4, FEATS, SHARD), bf16),
        ),
        in_specs=[vmem, hbm] + [vmem] * 8,
        out_specs=(hbm, hbm, hbm),
        scratch_shapes=[
            pltpu.VMEM((8, SHARD, SHARD), bf16),
            pltpu.VMEM((4, ROWS, FEATS), bf16),
            pltpu.VMEM((3, ROWS, SHARD), bf16),
            pltpu.VMEM((CHUNK, SHARD), bf16),
            pltpu.VMEM((ROWS, SHARD), bf16),
            pltpu.VMEM((ROWS, SHARD), bf16),
            pltpu.VMEM((ROWS, SHARD), bf16),
            pltpu.VMEM((1, ROWS), jnp.float32),
            pltpu.VMEM((FEATS, SHARD), bf16),
            dma((6, 9)),
            dma((6, 9)),
            dma((4, STEPS)),
            dma((4, STEPS)),
            dma((4, STEPS)),
            dma((3, STEPS)),
            dma((3,)),
            dma((3,)),
            dma((7,)),
        ],
        compiler_params=pltpu.CompilerParams(
            collective_id=0, has_side_effects=True, vmem_limit_bytes=60 * 2**20
        ),
    )(
        token_ids,
        section_outputs.reshape(ROWS, FEATS),
        *(w.reshape(SHARD, SHARD) for w in weights),
    )
    wide = jax.ShapeDtypeStruct((1, 1, ROWS, SHARD), jnp.float32)
    return pl.pallas_call(
        place_blocks,
        grid=(STEPS,),
        out_shape=(wide,) * 8 + (jax.ShapeDtypeStruct((1, 1, ROWS, FEATS), bf16),),
        in_specs=[
            pl.BlockSpec(memory_space=pltpu.SMEM),
            pl.BlockSpec((8, CHUNK, SHARD), lambda i: (0, i, 0)),
            pl.BlockSpec((4, CHUNK, SHARD), lambda i: (0, i, 0)),
            pl.BlockSpec((4, FEATS, SHARD), lambda i: (0, 0, 0)),
        ],
        out_specs=[pl.BlockSpec((1, 1, CHUNK, SHARD), lambda i: (0, 0, i, 0))] * 8
        + [pl.BlockSpec((1, 1, CHUNK, FEATS), lambda i: (0, 0, i, 0))],
        compiler_params=pltpu.CompilerParams(vmem_limit_bytes=60 * 2**20),
    )(failed_section, full, ctx, wo_rows)


def solution(mesh):
    stack = P("section", "dp", "tensor")
    block = P("dp", "section", None, "tensor")
    return jax.shard_map(
        shards,
        mesh=mesh,
        in_specs=(P("dp"), P("dp", None), block) + (stack,) * 8,
        out_specs=(block,) * 9,
        check_vma=False,
    )
```

time: 303 us -> 129 us (0.43)
  waiting for transfers between devices: 187 us -> 0 us
  Pallas kernels: 0 us -> 128 us
  matrix products: 56.7 us -> 0 us
  other arithmetic: 21.1 us -> 0 us
  local copies, waits for them, and re-layouts: 13.9 us -> 0 us
  between operations: 14.6 us -> 1.3 us
  starting transfers between devices: 6.04 us -> 0 us
    all_gather x4 -> x0, waiting for transfers between devices: 139 us -> none  [the longest x1 79.1 us: shards(): lax.all_gather(incoming, 'tensor', axis=3, tiled=True)[0, 0]]
    pallas_call x0 -> x2, Pallas kernels: none -> 128 us  [the longest x1 114 us: shards(): pl.pallas_call(gather_attend, out_shape=(jax.ShapeDtypeStruct((8, ROWS, S...]
    ppermute x1 -> x0, waiting for transfers between devices: 47 us -> none  [passed_along(): lax.ppermute(array, axis, [(i, (i + by) % count) for i in range(count)])]
    dot_general x6 -> x0, matrix products: 35.9 us -> none  [the longest x4 20.9 us: one_block(): jnp.einsum('hqk,khd->qhd', probs, value_heads, preferred_element_type=jnp...]
    sub x4 -> x0, matrix products: 20.8 us -> none  [one_block(): weights = jnp.exp(scores - highest)]
    select_n x2 -> x0, other arithmetic: 11.3 us -> none  [placed(): return jnp.where(replacing, gathered[None], jnp.zeros_like(gathered[None]))]
    convert_element_type x9 -> x0, other arithmetic: 4.01 us -> none  [the longest x1 1.04 us: shards(): w_query.astype(jnp.bfloat16)]
    all_to_all x1 -> x0, starting transfers between devices: 3.7 us -> none  [shards(): lax.all_to_all(out_bf, 'tensor', split_axis=0, concat_axis=1, tiled=True)]
  transfers between devices with their start and end apart: 6 -> 0, of which waited for: 5 -> 0; matrix products, arithmetic and copies ran while one was open for 26% -> 0% of each run, Pallas kernels for 0% -> 0%
where the time goes in v1:
time: 129 us
  Pallas kernels  128 us (99%)
  between operations  1.3 us (1%)
    pallas_call x1, Pallas kernels, shards(): pl.pallas_call(gather_attend, out_shape=(jax.ShapeDtypeStruct((8, ROWS, S...  114 us
    pallas_call x1, Pallas kernels, shards(): pl.pallas_call(place_blocks, grid=(STEPS,), out_shape=(wide,) * 8 + (jax....  13.9 us

profile of v1, /device:TPU:1, one launch (start us, length us, event | category | flops | bytes accessed | tf_op | source)
XLA Modules:
  0.0 128.8 jit_solution(10624817465490696368)
XLA Ops:
  1.3 113.6 %shard_map.178 = (bf16[8,2048,256]{2,1,0:T(8,128)(2,1)}, bf16[4,2048,256]{2,1,0:T(8,128)(2,1)}, bf16[4,512,256]{2,1,0:T(8,128)(2,1)}) custom-call(s32[1,2048]{1,0:T(1,128)} %tok.1, bf16[2048,512]{1,0:T(8,128)(2,1)} %bitcast.9, f32[256,256]{1,0:T(8,128)} %bitcast.10, f32[256,256]{1,0:T(8,128)} %bitcast.11, f32[256,256]{1,0:T(8,128)} %bitcast.12, ...), custom_call_target="tpu_custom_call" | custom-call | tf_op jit(solution)/shard_map/pallas_call | solution.py:299
  114.9 13.9 %shard_map.179 = (f32[1,1,2048,256]{3,2,1,0:T(8,128)}, f32[1,1,2048,256]{3,2,1,0:T(8,128)}, f32[1,1,2048,256]{3,2,1,0:T(8,128)}, f32[1,1,2048,256]{3,2,1,0:T(8,1...) custom-call(s32[1]{0:T(128)S(6)} %copy.20.failed, ...), custom_call_target="tpu_custom_call" | custom-call | tf_op jit(solution)/shard_map/pallas_call | solution.py:337

commit v2 on v1

v2 whole, which is shorter than its diff:
```python
import math

import jax
import jax.numpy as jnp
from jax import lax
from jax.experimental import pallas as pl
from jax.experimental.pallas import tpu as pltpu
from jax.sharding import PartitionSpec as P

MESH = pl.DeviceIdType.MESH
HD = 128
END_TOKEN = 100001
FILL = -1e30
SCALE = 1.0 / math.sqrt(HD)

ROWS = 2048
CHUNK = 256
STEPS = ROWS // CHUNK
SHARD = 256
FEATS = 512
HALF = SHARD // 2

GROUPS = ((0, 3), (3, 1), (4, 1), (5, 1), (6, 1), (7, 1))
LAST = 9


def produced(i):
    return jnp.clip(jnp.maximum(3 * i - 10, 0) // 2, 0, STEPS)


def gather_attend(
    failed, tok, x, wq, wk, wv, wo, mv, vv, mo, vo,
    full, ctx_full, wo_rows,
    xs, early, swap, qb, kb, vb, ends,
    w_send, w_recv, x_send, x_recv, c_send, c_recv, o_send, o_recv, local_sem,
):
    r = lax.axis_index("dp")
    s = lax.axis_index("section")
    t = lax.axis_index("tensor")
    zh, xi = r // 4, r % 4
    right = zh * 4 + (xi + 1) % 4
    left = zh * 4 + (xi + 3) % 4
    twin = (r + 4) % 8
    down = (s + 1) % 4
    up = (s + 3) % 4
    core = (t // 2) * 2 + (t + 1) % 2
    pair = (t + 2) % 4
    cross = (core + 2) % 4
    source = lax.rem(failed[0] + 3, 4) == s

    def rows(c):
        return pl.ds(pl.multiple_of(c * CHUNK, CHUNK), CHUNK)

    loads = [
        pltpu.make_async_copy(x.at[rows(2 * m + 1), :], early.at[m], local_sem.at[m])
        for m in range(STEPS // 2)
    ]
    for load in loads:
        load.start()
    for index, ref in enumerate((wq, wk, wv, wo, mv, vv, mo, vo)):
        full[index, pl.ds(pl.multiple_of(r * SHARD, SHARD), SHARD), :] = ref[...].astype(jnp.bfloat16)

    barrier = pltpu.get_barrier_semaphore()
    peers = (
        {"dp": right}, {"dp": left}, {"dp": twin}, {"section": down}, {"section": up},
        {"tensor": core}, {"tensor": pair}, {"tensor": cross},
    )
    for peer in peers:
        pl.semaphore_signal(barrier, inc=1, device_id=peer, device_id_type=MESH)
    pl.semaphore_wait(barrier, len(peers))

    def remote(src, dst, send, recv, to):
        return pltpu.make_async_remote_copy(
            src_ref=src, dst_ref=dst, send_sem=send, recv_sem=recv, device_id=to, device_id_type=MESH
        )

    def w_copy(g, kind):
        start, n = GROUPS[g]
        block = (r, r, r, twin, twin, left, right, (left + 4) % 8, (right + 4) % 8)[kind]
        to = (twin, right, left, right, left, right, left, right, left)[kind]
        first = HALF if kind in (6, 8) else 0
        count = HALF if kind >= 5 else SHARD
        part = full.at[pl.ds(start, n), pl.ds(pl.multiple_of(block * SHARD + first, HALF), count), :]
        return remote(part, part, w_send.at[g, kind], w_recv.at[g, kind], {"dp": to})

    def w_own(g):
        for kind in (0, 1, 2):
            w_copy(g, kind).start()

    def w_twin(g):
        w_copy(g, 0).wait_recv()
        w_copy(g, 3).start()
        w_copy(g, 4).start()

    def w_on(g):
        for kind in (1, 2):
            w_copy(g, kind).wait_recv()
            w_copy(g, kind + 4).start()

    def w_twin_on(g):
        for kind in (3, 4):
            w_copy(g, kind).wait_recv()
            w_copy(g, kind + 4).start()

    def w_whole(g):
        for kind in (5, 6, 7, 8):
            w_copy(g, kind).wait_recv()

    def x_copy(c, kind):
        sems = x_send.at[kind, c], x_recv.at[kind, c]
        if kind == 0:
            return remote(x.at[rows(c), :], xs.at[t, rows(c), :], *sems, {"section": down})
        if kind == 1:
            return remote(swap.at[c // 2], xs.at[t, rows(c), :], *sems, {"tensor": pair})
        if kind == 4:
            return remote(xs.at[pair, rows(c - 1), :], xs.at[pair, rows(c), :], *sems, {"section": down})
        part = xs.at[t if kind == 2 else pair, rows(c), :]
        return remote(part, part, *sems, {"tensor": core})

    def x_own(c):
        x_copy(c, 0).start()

    def x_wait(c):
        x_copy(c, 0).wait_recv()

    def x_share(c):
        x_copy(c, 2).start()

    def x_swap(c):
        loads[c // 2].wait()
        swap[c // 2] = jnp.where(source, early[c // 2], xs[t, rows(c), :])

    def x_swap_send(c):
        x_copy(c, 1).start()

    def x_swapped(c):
        x_copy(c, 1).wait_recv()
        x_copy(c + 1, 4).start()
        x_copy(c, 3).start()

    def x_other(c):
        x_copy(c, 4).wait_recv()
        x_copy(c, 3).start()

    def c_copy(c, kind):
        sems = c_send.at[kind, c], c_recv.at[kind, c]
        part = ctx_full.at[pair if kind == 2 else t, rows(c), :]
        return remote(part, part, *sems, {"tensor": pair if kind == 0 else core})

    def o_copy(kind):
        to = (pair, core, cross)[kind]
        src = full.at[3, pl.ds(pl.multiple_of(to * FEATS, FEATS), FEATS), :]
        return remote(src, wo_rows.at[t], o_send.at[kind], o_recv.at[kind], {"tensor": to})

    def o_all(_):
        w_whole(1)
        for kind in range(3):
            o_copy(kind).start()
        wo_rows[t] = full[3, pl.ds(pl.multiple_of(t * FEATS, FEATS), FEATS), :]

    where = lax.broadcasted_iota(jnp.int32, (1, ROWS), 1).astype(jnp.float32)
    ends[...] = jnp.where(tok[...] == END_TOKEN, where + 1.0, 0.0)

    def attend(c, _):
        for kind in (2, 3):
            x_copy(c, kind).wait_recv()
        for a, dst in enumerate((qb, kb, vb)):
            total = jnp.zeros((CHUNK, SHARD), jnp.float32)
            for part in range(4):
                total += jnp.dot(
                    xs[part, rows(c), :], full[a, part * FEATS : (part + 1) * FEATS, :],
                    preferred_element_type=jnp.float32,
                )
            if a == 0:
                dst[...] = total.astype(jnp.bfloat16)
            else:
                dst[rows(c), :] = total.astype(jnp.bfloat16)
        row = (c * CHUNK + lax.broadcasted_iota(jnp.int32, (CHUNK, 1), 0)).astype(jnp.float32)
        first = jnp.max(jnp.where(where < row, ends[...], 0.0), axis=1, keepdims=True)

        def step(j, carry):
            col = (j * CHUNK + lax.broadcasted_iota(jnp.int32, (1, CHUNK), 1)).astype(jnp.float32)
            allowed = (col <= row) & (col >= first)
            new = []
            for h in range(2):
                highest, total, acc = carry[h]
                lanes = slice(h * HD, (h + 1) * HD)
                scores = lax.dot_general(
                    qb[:, lanes], kb[rows(j), lanes], (((1,), (1,)), ((), ())),
                    preferred_element_type=jnp.float32,
                ) * SCALE
                scores = jnp.where(allowed, scores, FILL)
                top = jnp.maximum(highest, jnp.max(scores, axis=1, keepdims=True))
                weights = jnp.exp(scores - top)
                shrink = jnp.exp(highest - top)
                total = total * shrink + jnp.sum(weights, axis=1, keepdims=True)
                acc = acc * shrink + jnp.dot(
                    weights.astype(jnp.bfloat16), vb[rows(j), lanes], preferred_element_type=jnp.float32
                )
                new.append((top, total, acc))
            return tuple(new)

        begin = (
            jnp.full((CHUNK, 1), FILL, jnp.float32),
            jnp.zeros((CHUNK, 1), jnp.float32),
            jnp.zeros((CHUNK, HD), jnp.float32),
        )
        done = lax.fori_loop(0, c + 1, step, (begin, begin))
        for h in range(2):
            _, total, acc = done[h]
            ctx_full[t, rows(c), h * HD : (h + 1) * HD] = (acc / total).astype(jnp.bfloat16)
        return 0

    def send_context(c, _):
        c_copy(c, 0).start()
        c_copy(c, 1).start()
        return 0

    before = {
        1: [(w_twin, 0), (w_on, 0), (w_own, 3), (x_swapped, 0), (x_own, 3), (x_own, 4)],
        2: [],
        3: [(w_twin_on, 0), (w_twin, 1), (w_on, 2), (x_swapped, 2), (x_own, 5), (x_own, 6), (w_own, 5)],
        4: [],
        5: [(w_twin_on, 1), (w_twin, 4), (w_on, 4), (x_swapped, 4), (x_own, 7)],
        6: [(x_other, 3)],
        7: [(x_swapped, 6), (w_twin_on, 3), (o_all, 0)],
        8: [(x_other, 5)],
        9: [(w_twin_on, 4), (w_twin_on, 5), (x_other, 7)],
    }
    for c in range(STEPS):
        if c % 2 == 0:
            before[c] = [(x_wait, c), (x_swap, c), (x_share, c)] + before.get(c, [])
    before[0] += [(x_swap_send, 0), (w_own, 1), (w_own, 2)]
    before[2] += [(x_swap_send, 2), (w_on, 1), (w_own, 4)]
    before[4] += [(x_swap_send, 4), (x_other, 1), (w_on, 3), (w_twin, 2), (w_twin, 3), (w_whole, 0)]
    before[6] += [(x_swap_send, 6), (w_on, 5), (w_twin_on, 2), (w_twin, 5)]
    after = {c: [(x_wait, c), (x_share, c)] for c in range(1, STEPS, 2)}

    def run(i, table):
        for at, todo in table.items():
            @pl.when(i == at)
            def _(todo=todo):
                for act, what in todo:
                    act(what)

    w_own(0)
    for c in range(3):
        x_own(c)

    def loop(i, _):
        run(i, before)
        lax.fori_loop(produced(i - 2), produced(i - 1), send_context, 0)
        lax.fori_loop(produced(i - 1), produced(i), attend, 0)
        run(i, after)
        return 0

    lax.fori_loop(0, LAST + 1, loop, 0)

    def forward_context(c, _):
        c_copy(c, 0).wait_recv()
        c_copy(c, 2).start()
        return 0

    w_whole(2)
    lax.fori_loop(produced(LAST - 1), STEPS, send_context, 0)
    lax.fori_loop(0, STEPS, forward_context, 0)
    for g in range(3, 6):
        w_whole(g)
    for kind in range(3):
        o_copy(kind).wait()

    def finish(c, _):
        for kind in (0, 2, 3):
            x_copy(c, kind).wait_send()
        c_copy(c, 0).wait_send()
        c_copy(c, 1).wait()
        c_copy(c, 2).wait()
        return 0

    lax.fori_loop(0, STEPS, finish, 0)
    for c in range(0, STEPS, 2):
        x_copy(c, 1).wait_send()
        x_copy(c + 1, 4).wait_send()
    for g in range(6):
        for kind in range(9):
            w_copy(g, kind).wait_send()


def place_blocks(failed, full, ctx, wo_rows, *outs):
    replacing = lax.rem(failed[0], 4) == lax.axis_index("section")
    here = pl.ds(pl.multiple_of(pl.program_id(0) * CHUNK, CHUNK), CHUNK)
    for a in range(8):
        outs[a][0, 0] = jnp.where(replacing, full[a, here, :].astype(jnp.float32), 0.0)
    total = jnp.zeros((CHUNK, FEATS), jnp.float32)
    for part in range(4):
        total += lax.dot_general(
            ctx[part, here, :], wo_rows[part], (((1,), (1,)), ((), ())), preferred_element_type=jnp.float32
        )
    outs[8][0, 0] = jnp.where(replacing, total, 0.0).astype(jnp.bfloat16)


def shards(failed_section, token_ids, section_outputs, *weights):
    bf16 = jnp.bfloat16
    vmem = pl.BlockSpec(memory_space=pltpu.VMEM)
    hbm = pl.BlockSpec(memory_space=pl.ANY)
    dma = pltpu.SemaphoreType.DMA
    full, ctx, wo_rows = pl.pallas_call(
        gather_attend,
        out_shape=(
            pltpu.VMEM((8, ROWS, SHARD), bf16),
            pltpu.VMEM((4, ROWS, SHARD), bf16),
            pltpu.VMEM((4, FEATS, SHARD), bf16),
        ),
        in_specs=[pl.BlockSpec(memory_space=pltpu.SMEM), vmem, hbm] + [vmem] * 8,
        out_specs=(vmem, vmem, vmem),
        scratch_shapes=[
            pltpu.VMEM((4, ROWS, FEATS), bf16),
            pltpu.VMEM((STEPS // 2, CHUNK, FEATS), bf16),
            pltpu.VMEM((STEPS // 2, CHUNK, FEATS), bf16),
            pltpu.VMEM((CHUNK, SHARD), bf16),
            pltpu.VMEM((ROWS, SHARD), bf16),
            pltpu.VMEM((ROWS, SHARD), bf16),
            pltpu.VMEM((1, ROWS), jnp.float32),
            dma((6, 9)),
            dma((6, 9)),
            dma((5, STEPS)),
            dma((5, STEPS)),
            dma((3, STEPS)),
            dma((3, STEPS)),
            dma((3,)),
            dma((3,)),
            dma((STEPS // 2,)),
        ],
        compiler_params=pltpu.CompilerParams(
            collective_id=0, has_side_effects=True, vmem_limit_bytes=44 * 2**20
        ),
    )(
        failed_section,
        token_ids,
        section_outputs.reshape(ROWS, FEATS),
        *(w.reshape(SHARD, SHARD) for w in weights),
    )
    wide = jax.ShapeDtypeStruct((1, 1, ROWS, SHARD), jnp.float32)
    return pl.pallas_call(
        place_blocks,
        grid=(STEPS,),
        out_shape=(wide,) * 8 + (jax.ShapeDtypeStruct((1, 1, ROWS, FEATS), bf16),),
        in_specs=[
            pl.BlockSpec(memory_space=pltpu.SMEM),
            vmem,
            vmem,
            vmem,
        ],
        out_specs=[pl.BlockSpec((1, 1, CHUNK, SHARD), lambda i: (0, 0, i, 0))] * 8
        + [pl.BlockSpec((1, 1, CHUNK, FEATS), lambda i: (0, 0, i, 0))],
        compiler_params=pltpu.CompilerParams(vmem_limit_bytes=24 * 2**20),
    )(failed_section, full, ctx, wo_rows)


def solution(mesh):
    stack = P("section", "dp", "tensor")
    block = P("dp", "section", None, "tensor")
    return jax.shard_map(
        shards,
        mesh=mesh,
        in_specs=(P("dp"), P("dp", None), block) + (stack,) * 8,
        out_specs=(block,) * 9,
        check_vma=False,
    )
```

time: 129 us -> 115 us (0.89)
  Pallas kernels: 128 us -> 113 us
    pallas_call x1, Pallas kernels: 114 us -> 106 us  [shards(): pl.pallas_call(gather_attend, out_shape=(pltpu.VMEM((8, ROWS, SHARD), bf1...]
    pallas_call x1, Pallas kernels: 13.9 us -> 7.92 us  [shards(): pl.pallas_call(place_blocks, grid=(STEPS,), out_shape=(wide,) * 8 + (jax....]
where the time goes in v2:
time: 115 us
  Pallas kernels  113 us (98%)
  between operations  1.3 us (1%)
    pallas_call x1, Pallas kernels, shards(): pl.pallas_call(gather_attend, out_shape=(pltpu.VMEM((8, ROWS, SHARD), bf1...  106 us
    pallas_call x1, Pallas kernels, shards(): pl.pallas_call(place_blocks, grid=(STEPS,), out_shape=(wide,) * 8 + (jax....  7.92 us

profile of v2, /device:TPU:1, one launch (start us, length us, event | category | flops | bytes accessed | tf_op | source)
XLA Modules:
  0.0 114.7 jit_solution(5034046816085869666)
XLA Ops:
  1.3 105.5 %shard_map.178 = (bf16[8,2048,256]{2,1,0:T(8,128)(2,1)S(1)}, bf16[4,2048,256]{2,1,0:T(8,128)(2,1)S(1)}, bf16[4,512,256]{2,1,0:T(8,128)(2,1)S(1)}) custom-call(s32[1]{0:T(128)S(6)} %copy.20.failed, s32[1,2048]{1,0:T(1,128)} %tok.1, bf16[2048,512]{1,0:T(8,128)(2,1)} %bitcast.9, f32[256,256]{1,0:T(8,128)} %bitcast.10, f32[256,256]{1,0:T(8,128)} %bitcast.11, ...), custom_call_target="tpu_custom_call" | custom-call | tf_op jit(solution)/shard_map/pallas_call | solution.py:307
  106.8 7.9 %shard_map.179 = (f32[1,1,2048,256]{3,2,1,0:T(8,128)}, f32[1,1,2048,256]{3,2,1,0:T(8,128)}, f32[1,1,2048,256]{3,2,1,0:T(8,128)}, f32[1,1,2048,256]{3,2,1,0:T(8,1...) custom-call(s32[1]{0:T(128)S(6)} %copy.20.failed, ...), custom_call_target="tpu_custom_call" | custom-call | tf_op jit(solution)/shard_map/pallas_call | solution.py:344

commit v3 on v2

--- a/solution.py
+++ b/solution.py
@@ -22,16 +22,19 @@
 
 GROUPS = ((0, 3), (3, 1), (4, 1), (5, 1), (6, 1), (7, 1))
 LAST = 9
+LATE = (0, 1, 3, 5)
+EARLY = (2, 4, 6, 7)
+VIA = (0, 2, 4)
 
 
 def produced(i):
-    return jnp.clip(jnp.maximum(3 * i - 10, 0) // 2, 0, STEPS)
+    return jnp.clip(jnp.minimum(2 * (i - 4), i - 1), 0, STEPS)
 
 
 def gather_attend(
     failed, tok, x, wq, wk, wv, wo, mv, vv, mo, vo,
     full, ctx_full, wo_rows,
-    xs, early, swap, qb, kb, vb, ends,
+    xs, early, swap, back, lent, cswap, olent, oswap, oback, qb, kb, vb, ends,
     w_send, w_recv, x_send, x_recv, c_send, c_recv, o_send, o_recv, local_sem,
 ):
     r = lax.axis_index("dp")
@@ -52,8 +55,8 @@
         return pl.ds(pl.multiple_of(c * CHUNK, CHUNK), CHUNK)
 
     loads = [
-        pltpu.make_async_copy(x.at[rows(2 * m + 1), :], early.at[m], local_sem.at[m])
-        for m in range(STEPS // 2)
+        pltpu.make_async_copy(x.at[rows(c), :], early.at[k], local_sem.at[k])
+        for k, c in enumerate(EARLY + LATE[3:])
     ]
     for load in loads:
         load.start()
@@ -111,12 +114,19 @@
         if kind == 0:
             return remote(x.at[rows(c), :], xs.at[t, rows(c), :], *sems, {"section": down})
         if kind == 1:
-            return remote(swap.at[c // 2], xs.at[t, rows(c), :], *sems, {"tensor": pair})
+            return remote(swap.at[LATE.index(c)], xs.at[t, rows(c), :], *sems, {"tensor": pair})
         if kind == 4:
-            return remote(xs.at[pair, rows(c - 1), :], xs.at[pair, rows(c), :], *sems, {"section": down})
+            met = xs.at[pair, rows(LATE[EARLY.index(c)]), :]
+            return remote(met, xs.at[pair, rows(c), :], *sems, {"section": down})
         part = xs.at[t if kind == 2 else pair, rows(c), :]
         return remote(part, part, *sems, {"tensor": core})
 
+    def b_copy(j):
+        third, fourth = xs.at[t, rows(LATE[2]), :], xs.at[t, rows(LATE[3]), :]
+        src = (x.at[rows(LATE[2]), :], swap.at[4], back.at[1], third)[j]
+        dst = (back.at[0], back.at[1], third, fourth)[j]
+        return remote(src, dst, x_send.at[5, j], x_recv.at[5, j], {"section": up})
+
     def x_own(c):
         x_copy(c, 0).start()
 
@@ -127,36 +137,102 @@
         x_copy(c, 2).start()
 
     def x_swap(c):
-        loads[c // 2].wait()
-        swap[c // 2] = jnp.where(source, early[c // 2], xs[t, rows(c), :])
+        k = LATE.index(c)
+        loads[k].wait()
+        swap[k] = jnp.where(source, early[k], xs[t, rows(c), :])
 
     def x_swap_send(c):
         x_copy(c, 1).start()
 
     def x_swapped(c):
         x_copy(c, 1).wait_recv()
-        x_copy(c + 1, 4).start()
+        x_copy(EARLY[LATE.index(c)], 4).start()
         x_copy(c, 3).start()
 
     def x_other(c):
         x_copy(c, 4).wait_recv()
         x_copy(c, 3).start()
 
+    def b_wait(j):
+        b_copy(j).wait_recv()
+
+    def b_send(j):
+        b_copy(j).start()
+
+    def b_choose(_):
+        loads[4].wait()
+        swap[4] = jnp.where(source, early[4], back[0])
+
     def c_copy(c, kind):
         sems = c_send.at[kind, c], c_recv.at[kind, c]
-        part = ctx_full.at[pair if kind == 2 else t, rows(c), :]
-        return remote(part, part, *sems, {"tensor": pair if kind == 0 else core})
+        mine, other = ctx_full.at[t, rows(c), :], ctx_full.at[pair, rows(c), :]
+        if kind == 3:
+            return remote(mine, lent.at[VIA.index(c)], *sems, {"section": up})
+        if kind == 4:
+            return remote(ctx_full.at[pair, rows(c + 1), :], other, *sems, {"section": down})
+        if kind == 2:
+            return remote(other, other, *sems, {"tensor": core})
+        if kind == 0 and c - 1 in VIA:
+            return remote(cswap.at[VIA.index(c - 1)], mine, *sems, {"tensor": pair})
+        return remote(mine, mine, *sems, {"tensor": pair if kind == 0 else core})
+
+    def c_done(c):
+        c_copy(c, 1).start()
+        if c in VIA:
+            c_copy(c, 3).start()
+        elif c - 1 not in VIA:
+            c_copy(c, 0).start()
+
+    def c_swap(c):
+        k = VIA.index(c)
+        c_copy(c, 3).wait_recv()
+        cswap[k] = jnp.where(source, lent[k], ctx_full[t, rows(c + 1), :])
+
+    def c_swap_send(c):
+        c_copy(c + 1, 0).start()
+
+    def c_swapped(c):
+        c_copy(c + 1, 0).wait_recv()
+        c_copy(c, 4).start()
+        c_copy(c + 1, 2).start()
+
+    def c_back(c):
+        c_copy(c, 4).wait_recv()
+        c_copy(c, 2).start()
+
+    def o_rows(owner):
+        return pl.ds(pl.multiple_of(owner * FEATS, FEATS), FEATS)
 
     def o_copy(kind):
-        to = (pair, core, cross)[kind]
-        src = full.at[3, pl.ds(pl.multiple_of(to * FEATS, FEATS), FEATS), :]
-        return remote(src, wo_rows.at[t], o_send.at[kind], o_recv.at[kind], {"tensor": to})
-
-    def o_all(_):
+        src, dst, to = (
+            (full.at[3, o_rows(core), :], wo_rows.at[t], {"tensor": core}),
+            (full.at[3, o_rows(cross), :], olent, {"section": up}),
+            (oswap, wo_rows.at[t], {"tensor": pair}),
+            (wo_rows.at[pair], oback, {"section": down}),
+            (oback, wo_rows.at[pair], {"tensor": core}),
+        )[kind]
+        return remote(src, dst, o_send.at[kind], o_recv.at[kind], to)
+
+    def o_first(_):
         w_whole(1)
-        for kind in range(3):
-            o_copy(kind).start()
-        wo_rows[t] = full[3, pl.ds(pl.multiple_of(t * FEATS, FEATS), FEATS), :]
+        o_copy(1).start()
+        o_copy(0).start()
+        wo_rows[t] = full[3, o_rows(t), :]
+
+    def o_swap(_):
+        o_copy(1).wait_recv()
+        oswap[...] = jnp.where(source, olent[...], full[3, o_rows(pair), :])
+
+    def o_swap_send(_):
+        o_copy(2).start()
+
+    def o_swapped(_):
+        o_copy(2).wait_recv()
+        o_copy(3).start()
+
+    def o_back(_):
+        o_copy(3).wait_recv()
+        o_copy(4).start()
 
     where = lax.broadcasted_iota(jnp.int32, (1, ROWS), 1).astype(jnp.float32)
     ends[...] = jnp.where(tok[...] == END_TOKEN, where + 1.0, 0.0)
@@ -211,30 +287,44 @@
             ctx_full[t, rows(c), h * HD : (h + 1) * HD] = (acc / total).astype(jnp.bfloat16)
         return 0
 
-    def send_context(c, _):
-        c_copy(c, 0).start()
-        c_copy(c, 1).start()
-        return 0
-
     before = {
-        1: [(w_twin, 0), (w_on, 0), (w_own, 3), (x_swapped, 0), (x_own, 3), (x_own, 4)],
-        2: [],
-        3: [(w_twin_on, 0), (w_twin, 1), (w_on, 2), (x_swapped, 2), (x_own, 5), (x_own, 6), (w_own, 5)],
-        4: [],
-        5: [(w_twin_on, 1), (w_twin, 4), (w_on, 4), (x_swapped, 4), (x_own, 7)],
-        6: [(x_other, 3)],
-        7: [(x_swapped, 6), (w_twin_on, 3), (o_all, 0)],
-        8: [(x_other, 5)],
-        9: [(w_twin_on, 4), (w_twin_on, 5), (x_other, 7)],
+        0: [
+            (x_wait, 0), (x_swap, 0), (x_share, 0), (b_wait, 0), (b_choose, 0), (x_swap_send, 0),
+            (w_own, 1), (b_send, 1),
+        ],
+        1: [
+            (w_twin, 0), (w_on, 0), (x_wait, 1), (x_swap, 1), (x_share, 1),
+            (b_wait, 1), (b_send, 2), (x_swap_send, 1),
+        ],
+        2: [(x_swapped, 0), (x_own, 6), (w_twin, 1), (w_on, 1), (x_wait, 2), (x_share, 2)],
+        3: [
+            (b_wait, 2), (b_send, 3), (x_swap, 3), (x_share, 3), (w_twin_on, 0),
+            (x_swap_send, 3), (w_own, 2), (w_own, 3),
+        ],
+        4: [(x_swapped, 1), (x_own, 7), (x_wait, 4), (x_share, 4), (w_twin_on, 1)],
+        5: [
+            (b_wait, 3), (x_swap, 5), (x_share, 5), (w_own, 4), (x_swap_send, 5), (w_own, 5), (w_whole, 0),
+        ],
+        6: [
+            (x_swapped, 3), (x_other, 2), (c_done, 0), (c_done, 1), (x_wait, 6), (x_share, 6),
+            (w_on, 2), (w_twin, 2),
+        ],
+        7: [
+            (x_swapped, 5), (x_other, 4), (c_swap, 0), (c_done, 2), (c_done, 3), (c_swap_send, 0),
+            (o_first, 0), (w_on, 3), (w_twin, 3), (w_on, 4), (w_twin, 4), (x_wait, 7), (x_share, 7),
+        ],
+        8: [
+            (x_other, 6), (c_swap, 2), (o_swap, 0), (c_done, 4), (c_done, 5), (c_swap_send, 2), (o_swap_send, 0),
+            (c_swapped, 0), (w_on, 5), (w_twin, 5), (w_twin_on, 2),
+        ],
+        9: [
+            (x_other, 7), (c_swap, 4), (c_done, 6), (c_swap_send, 4), (c_swapped, 2), (o_swapped, 0),
+            (w_twin_on, 3), (c_back, 0),
+        ],
     }
-    for c in range(STEPS):
-        if c % 2 == 0:
-            before[c] = [(x_wait, c), (x_swap, c), (x_share, c)] + before.get(c, [])
-    before[0] += [(x_swap_send, 0), (w_own, 1), (w_own, 2)]
-    before[2] += [(x_swap_send, 2), (w_on, 1), (w_own, 4)]
-    before[4] += [(x_swap_send, 4), (x_other, 1), (w_on, 3), (w_twin, 2), (w_twin, 3), (w_whole, 0)]
-    before[6] += [(x_swap_send, 6), (w_on, 5), (w_twin_on, 2), (w_twin, 5)]
-    after = {c: [(x_wait, c), (x_share, c)] for c in range(1, STEPS, 2)}
+    tail = [
+        (w_twin_on, 4), (c_done, 7), (c_swapped, 4), (w_twin_on, 5), (c_back, 2), (o_back, 0),
+    ]
 
     def run(i, table):
         for at, todo in table.items():
@@ -244,43 +334,47 @@
                     act(what)
 
     w_own(0)
-    for c in range(3):
+    b_send(0)
+    for c in (0, 1, 2, 4):
         x_own(c)
 
     def loop(i, _):
         run(i, before)
-        lax.fori_loop(produced(i - 2), produced(i - 1), send_context, 0)
         lax.fori_loop(produced(i - 1), produced(i), attend, 0)
-        run(i, after)
         return 0
 
     lax.fori_loop(0, LAST + 1, loop, 0)
 
-    def forward_context(c, _):
+    for act, what in tail:
+        act(what)
+    for c in (6, 7):
         c_copy(c, 0).wait_recv()
         c_copy(c, 2).start()
+    c_back(4)
+    for g in range(2, 6):
+        w_whole(g)
+    for kind in (0, 4):
+        o_copy(kind).wait_recv()
+    for kind in range(5):
+        o_copy(kind).wait_send()
+    for c in range(STEPS):
+        for kind in (1, 2):
+            c_copy(c, kind).wait()
+        for kind in (3, 4) if c in VIA else (0,):
+            c_copy(c, kind).wait_send()
+
+    def finish(c, _):
+        for kind in (2, 3):
+            x_copy(c, kind).wait_send()
         return 0
 
-    w_whole(2)
-    lax.fori_loop(produced(LAST - 1), STEPS, send_context, 0)
-    lax.fori_loop(0, STEPS, forward_context, 0)
-    for g in range(3, 6):
-        w_whole(g)
-    for kind in range(3):
-        o_copy(kind).wait()
-
-    def finish(c, _):
-        for kind in (0, 2, 3):
-            x_copy(c, kind).wait_send()
-        c_copy(c, 0).wait_send()
-        c_copy(c, 1).wait()
-        c_copy(c, 2).wait()
-        return 0
-
     lax.fori_loop(0, STEPS, finish, 0)
-    for c in range(0, STEPS, 2):
-        x_copy(c, 1).wait_send()
-        x_copy(c + 1, 4).wait_send()
+    for c in EARLY + LATE[:2]:
+        x_copy(c, 0).wait_send()
+    for k in range(4):
+        x_copy(LATE[k], 1).wait_send()
+        x_copy(EARLY[k], 4).wait_send()
+        b_copy(k).wait_send()
     for g in range(6):
         for kind in range(9):
             w_copy(g, kind).wait_send()
@@ -315,21 +409,27 @@
         out_specs=(vmem, vmem, vmem),
         scratch_shapes=[
             pltpu.VMEM((4, ROWS, FEATS), bf16),
-            pltpu.VMEM((STEPS // 2, CHUNK, FEATS), bf16),
-            pltpu.VMEM((STEPS // 2, CHUNK, FEATS), bf16),
+            pltpu.VMEM((5, CHUNK, FEATS), bf16),
+            pltpu.VMEM((5, CHUNK, FEATS), bf16),
+            pltpu.VMEM((2, CHUNK, FEATS), bf16),
+            pltpu.VMEM((3, CHUNK, SHARD), bf16),
+            pltpu.VMEM((3, CHUNK, SHARD), bf16),
+            pltpu.VMEM((FEATS, SHARD), bf16),
+            pltpu.VMEM((FEATS, SHARD), bf16),
+            pltpu.VMEM((FEATS, SHARD), bf16),
             pltpu.VMEM((CHUNK, SHARD), bf16),
             pltpu.VMEM((ROWS, SHARD), bf16),
             pltpu.VMEM((ROWS, SHARD), bf16),
             pltpu.VMEM((1, ROWS), jnp.float32),
             dma((6, 9)),
             dma((6, 9)),
+            dma((6, STEPS)),
+            dma((6, STEPS)),
             dma((5, STEPS)),
             dma((5, STEPS)),
-            dma((3, STEPS)),
-            dma((3, STEPS)),
-            dma((3,)),
-            dma((3,)),
-            dma((STEPS // 2,)),
+            dma((5,)),
+            dma((5,)),
+            dma((5,)),
         ],
         compiler_params=pltpu.CompilerParams(
             collective_id=0, has_side_effects=True, vmem_limit_bytes=44 * 2**20

time: 115 us -> 106 us (0.922)
  Pallas kernels: 113 us -> 105 us
    pallas_call x1, Pallas kernels: 106 us -> 97 us  [shards(): pl.pallas_call(gather_attend, out_shape=(pltpu.VMEM((8, ROWS, SHARD), bf1...]
where the time goes in v3:
time: 106 us
  Pallas kernels  105 us (99%)
  between operations  1.3 us (1%)
    pallas_call x1, Pallas kernels, shards(): pl.pallas_call(gather_attend, out_shape=(pltpu.VMEM((8, ROWS, SHARD), bf1...  97 us
    pallas_call x1, Pallas kernels, shards(): pl.pallas_call(place_blocks, grid=(STEPS,), out_shape=(wide,) * 8 + (jax....  7.93 us

profile of v3, /device:TPU:1, one launch (start us, length us, event | category | flops | bytes accessed | tf_op | source)
XLA Modules:
  0.0 106.2 jit_solution(10374213877399095905)
XLA Ops:
  1.3 97.0 %shard_map.178 = (bf16[8,2048,256]{2,1,0:T(8,128)(2,1)S(1)}, bf16[4,2048,256]{2,1,0:T(8,128)(2,1)S(1)}, bf16[4,512,256]{2,1,0:T(8,128)(2,1)S(1)}) custom-call(s32[1]{0:T(128)S(6)} %copy.20.failed, s32[1,2048]{1,0:T(1,128)} %tok.1, bf16[2048,512]{1,0:T(8,128)(2,1)} %bitcast.9, f32[256,256]{1,0:T(8,128)} %bitcast.10, f32[256,256]{1,0:T(8,128)} %bitcast.11, ...), custom_call_target="tpu_custom_call" | custom-call | tf_op jit(solution)/shard_map/pallas_call | solution.py:401
  98.3 7.9 %shard_map.179 = (f32[1,1,2048,256]{3,2,1,0:T(8,128)}, f32[1,1,2048,256]{3,2,1,0:T(8,128)}, f32[1,1,2048,256]{3,2,1,0:T(8,128)}, f32[1,1,2048,256]{3,2,1,0:T(8,1...) custom-call(s32[1]{0:T(128)S(6)} %copy.20.failed, ...), custom_call_target="tpu_custom_call" | custom-call | tf_op jit(solution)/shard_map/pallas_call | solution.py:444

commit v4 on v3

--- a/solution.py
+++ b/solution.py
@@ -11,7 +11,7 @@
 HD = 128
 END_TOKEN = 100001
 FILL = -1e30
-SCALE = 1.0 / math.sqrt(HD)
+SCALE_LOG2 = math.log2(math.e) / math.sqrt(HD)
 
 ROWS = 2048
 CHUNK = 256
@@ -19,6 +19,7 @@
 SHARD = 256
 FEATS = 512
 HALF = SHARD // 2
+BAND = 512
 
 GROUPS = ((0, 3), (3, 1), (4, 1), (5, 1), (6, 1), (7, 1))
 LAST = 9
@@ -35,6 +36,7 @@
     failed, tok, x, wq, wk, wv, wo, mv, vv, mo, vo,
     full, ctx_full, wo_rows,
     xs, early, swap, back, lent, cswap, olent, oswap, oback, qb, kb, vb, ends,
+    sb, tops, sums, accs,
     w_send, w_recv, x_send, x_recv, c_send, c_recv, o_send, o_recv, local_sem,
 ):
     r = lax.axis_index("dp")
@@ -60,8 +62,12 @@
     ]
     for load in loads:
         load.start()
-    for index, ref in enumerate((wq, wk, wv, wo, mv, vv, mo, vo)):
-        full[index, pl.ds(pl.multiple_of(r * SHARD, SHARD), SHARD), :] = ref[...].astype(jnp.bfloat16)
+    sources = (wq, wk, wv, wo, mv, vv, mo, vo)
+
+    def rounded(first, last):
+        for index in range(first, last):
+            here = pl.ds(pl.multiple_of(r * SHARD, SHARD), SHARD)
+            full[index, here, :] = sources[index][...].astype(jnp.bfloat16)
 
     barrier = pltpu.get_barrier_semaphore()
     peers = (
@@ -70,6 +76,7 @@
     )
     for peer in peers:
         pl.semaphore_signal(barrier, inc=1, device_id=peer, device_id_type=MESH)
+    rounded(0, 3)
     pl.semaphore_wait(barrier, len(peers))
 
     def remote(src, dst, send, recv, to):
@@ -254,37 +261,44 @@
         row = (c * CHUNK + lax.broadcasted_iota(jnp.int32, (CHUNK, 1), 0)).astype(jnp.float32)
         first = jnp.max(jnp.where(where < row, ends[...], 0.0), axis=1, keepdims=True)
 
-        def step(j, carry):
+        def score(j, diagonal):
             col = (j * CHUNK + lax.broadcasted_iota(jnp.int32, (1, CHUNK), 1)).astype(jnp.float32)
-            allowed = (col <= row) & (col >= first)
-            new = []
+            allowed = col >= first
+            if diagonal:
+                allowed = allowed & (col <= row)
             for h in range(2):
-                highest, total, acc = carry[h]
                 lanes = slice(h * HD, (h + 1) * HD)
                 scores = lax.dot_general(
                     qb[:, lanes], kb[rows(j), lanes], (((1,), (1,)), ((), ())),
                     preferred_element_type=jnp.float32,
-                ) * SCALE
+                )
                 scores = jnp.where(allowed, scores, FILL)
-                top = jnp.maximum(highest, jnp.max(scores, axis=1, keepdims=True))
-                weights = jnp.exp(scores - top)
-                shrink = jnp.exp(highest - top)
-                total = total * shrink + jnp.sum(weights, axis=1, keepdims=True)
-                acc = acc * shrink + jnp.dot(
+                sb[h, j] = scores
+                top = jnp.maximum(scores[:, :HD], scores[:, HD:])
+                tops[h] = top if diagonal else jnp.maximum(tops[h], top)
+
+        def mix(j, highest, last):
+            for h in range(2):
+                lanes = slice(h * HD, (h + 1) * HD)
+                weights = jnp.exp2((sb[h, j] - highest[h]) * SCALE_LOG2)
+                total = weights[:, :HD] + weights[:, HD:]
+                acc = jnp.dot(
                     weights.astype(jnp.bfloat16), vb[rows(j), lanes], preferred_element_type=jnp.float32
                 )
-                new.append((top, total, acc))
-            return tuple(new)
-
-        begin = (
-            jnp.full((CHUNK, 1), FILL, jnp.float32),
-            jnp.zeros((CHUNK, 1), jnp.float32),
-            jnp.zeros((CHUNK, HD), jnp.float32),
-        )
-        done = lax.fori_loop(0, c + 1, step, (begin, begin))
-        for h in range(2):
-            _, total, acc = done[h]
-            ctx_full[t, rows(c), h * HD : (h + 1) * HD] = (acc / total).astype(jnp.bfloat16)
+                if last:
+                    total = jnp.sum(total + sums[h], axis=1, keepdims=True)
+                    ctx_full[t, rows(j), lanes] = ((acc + accs[h]) / total).astype(jnp.bfloat16)
+                else:
+                    sums[h] += total
+                    accs[h] += acc
+
+        score(c, True)
+        lax.fori_loop(0, c, lambda j, _: (score(j, False), 0)[1], 0)
+        highest = [jnp.max(tops[h], axis=1, keepdims=True) for h in range(2)]
+        sums[...] = jnp.zeros_like(sums)
+        accs[...] = jnp.zeros_like(accs)
+        lax.fori_loop(0, c, lambda j, _: (mix(j, highest, False), 0)[1], 0)
+        mix(c, highest, True)
         return 0
 
     before = {
@@ -337,6 +351,7 @@
     b_send(0)
     for c in (0, 1, 2, 4):
         x_own(c)
+    rounded(3, 8)
 
     def loop(i, _):
         run(i, before)
@@ -380,17 +395,46 @@
             w_copy(g, kind).wait_send()
 
 
-def place_blocks(failed, full, ctx, wo_rows, *outs):
+def place_blocks(failed, full, ctx, wo_rows, *rest):
+    outs, (wide, update, sems) = rest[:9], rest[9:]
     replacing = lax.rem(failed[0], 4) == lax.axis_index("section")
-    here = pl.ds(pl.multiple_of(pl.program_id(0) * CHUNK, CHUNK), CHUNK)
+
+    def rows(i):
+        return pl.ds(pl.multiple_of(i * BAND, BAND), BAND)
+
+    def out(a, i):
+        return pltpu.make_async_copy(wide.at[a, rows(i), :], outs[a].at[0, 0, rows(i), :], sems.at[a, i])
+
+    def out_update(i):
+        return pltpu.make_async_copy(update.at[rows(i), :], outs[8].at[0, 0, rows(i), :], sems.at[8, i])
+
     for a in range(8):
-        outs[a][0, 0] = jnp.where(replacing, full[a, here, :].astype(jnp.float32), 0.0)
-    total = jnp.zeros((CHUNK, FEATS), jnp.float32)
-    for part in range(4):
-        total += lax.dot_general(
-            ctx[part, here, :], wo_rows[part], (((1,), (1,)), ((), ())), preferred_element_type=jnp.float32
-        )
-    outs[8][0, 0] = jnp.where(replacing, total, 0.0).astype(jnp.bfloat16)
+        def widen(i, _, a=a):
+            wide[a, rows(i), :] = jnp.where(replacing, full[a, rows(i), :].astype(jnp.float32), 0.0)
+            out(a, i).start()
+            return 0
+
+        lax.fori_loop(0, ROWS // BAND, widen, 0)
+
+    def project(i, _):
+        total = jnp.zeros((BAND, FEATS), jnp.float32)
+        for part in range(4):
+            total += lax.dot_general(
+                ctx[part, rows(i), :], wo_rows[part], (((1,), (1,)), ((), ())), preferred_element_type=jnp.float32
+            )
+        update[rows(i), :] = jnp.where(replacing, total, 0.0).astype(jnp.bfloat16)
+        out_update(i).start()
+        return 0
+
+    lax.fori_loop(0, ROWS // BAND, project, 0)
+
+    def finish(i, _):
+        for a in range(8):
+            out(a, i).wait()
+        out_update(i).wait()
+        return 0
+
+    lax.fori_loop(0, ROWS // BAND, finish, 0)
 
 
 def shards(failed_section, token_ids, section_outputs, *weights):
@@ -421,6 +465,10 @@
             pltpu.VMEM((ROWS, SHARD), bf16),
             pltpu.VMEM((ROWS, SHARD), bf16),
             pltpu.VMEM((1, ROWS), jnp.float32),
+            pltpu.VMEM((2, STEPS, CHUNK, CHUNK), jnp.float32),
+            pltpu.VMEM((2, CHUNK, HD), jnp.float32),
+            pltpu.VMEM((2, CHUNK, HD), jnp.float32),
+            pltpu.VMEM((2, CHUNK, HD), jnp.float32),
             dma((6, 9)),
             dma((6, 9)),
             dma((6, STEPS)),
@@ -443,7 +491,6 @@
     wide = jax.ShapeDtypeStruct((1, 1, ROWS, SHARD), jnp.float32)
     return pl.pallas_call(
         place_blocks,
-        grid=(STEPS,),
         out_shape=(wide,) * 8 + (jax.ShapeDtypeStruct((1, 1, ROWS, FEATS), bf16),),
         in_specs=[
             pl.BlockSpec(memory_space=pltpu.SMEM),
@@ -451,8 +498,12 @@
             vmem,
             vmem,
         ],
-        out_specs=[pl.BlockSpec((1, 1, CHUNK, SHARD), lambda i: (0, 0, i, 0))] * 8
-        + [pl.BlockSpec((1, 1, CHUNK, FEATS), lambda i: (0, 0, i, 0))],
+        out_specs=[hbm] * 9,
+        scratch_shapes=[
+            pltpu.VMEM((8, ROWS, SHARD), jnp.float32),
+            pltpu.VMEM((ROWS, FEATS), bf16),
+            dma((9, ROWS // BAND)),
+        ],
         compiler_params=pltpu.CompilerParams(vmem_limit_bytes=24 * 2**20),
     )(failed_section, full, ctx, wo_rows)
 

time: 106 us -> 99.7 us (0.941)
  Pallas kernels: 105 us -> 98.2 us
    pallas_call x1, Pallas kernels: 97 us -> 91.4 us  [shards(): pl.pallas_call(gather_attend, out_shape=(pltpu.VMEM((8, ROWS, SHARD), bf1...]
    pallas_call x1, Pallas kernels: 7.93 us -> 6.79 us  [shards(): pl.pallas_call(place_blocks, out_shape=(wide,) * 8 + (jax.ShapeDtypeStruc...]
where the time goes in v4:
time: 99.7 us; the launch traced here: 99.5 us
  Pallas kernels  98.2 us (98%)
  between operations  1.3 us (1%)
    pallas_call x1, Pallas kernels, shards(): pl.pallas_call(gather_attend, out_shape=(pltpu.VMEM((8, ROWS, SHARD), bf1...  91.4 us
    pallas_call x1, Pallas kernels, shards(): pl.pallas_call(place_blocks, out_shape=(wide,) * 8 + (jax.ShapeDtypeStruc...  6.79 us

profile of v4, /device:TPU:1, one launch (start us, length us, event | category | flops | bytes accessed | tf_op | source)
XLA Modules:
  0.0 99.5 jit_solution(16138580111309357613)
XLA Ops:
  1.3 91.4 %shard_map.178 = (bf16[8,2048,256]{2,1,0:T(8,128)(2,1)S(1)}, bf16[4,2048,256]{2,1,0:T(8,128)(2,1)S(1)}, bf16[4,512,256]{2,1,0:T(8,128)(2,1)S(1)}) custom-call(s32[1]{0:T(128)S(6)} %copy.20.failed, s32[1,2048]{1,0:T(1,128)} %tok.1, bf16[2048,512]{1,0:T(8,128)(2,1)} %bitcast.9, f32[256,256]{1,0:T(8,128)} %bitcast.10, f32[256,256]{1,0:T(8,128)} %bitcast.11, ...), custom_call_target="tpu_custom_call" | custom-call | tf_op jit(solution)/shard_map/pallas_call | solution.py:445
  92.7 6.8 %shard_map.179 = (f32[1,1,2048,256]{3,2,1,0:T(8,128)}, f32[1,1,2048,256]{3,2,1,0:T(8,128)}, f32[1,1,2048,256]{3,2,1,0:T(8,128)}, f32[1,1,2048,256]{3,2,1,0:T(8,1...) custom-call(s32[1]{0:T(128)S(6)} %copy.20.failed, ...), custom_call_target="tpu_custom_call" | custom-call | tf_op jit(solution)/shard_map/pallas_call | solution.py:492

commit v5 on v4

--- a/solution.py
+++ b/solution.py
@@ -16,6 +16,7 @@
 ROWS = 2048
 CHUNK = 256
 STEPS = ROWS // CHUNK
+WIDE = 512
 SHARD = 256
 FEATS = 512
 HALF = SHARD // 2
@@ -25,6 +26,7 @@
 LAST = 9
 LATE = (0, 1, 3, 5)
 EARLY = (2, 4, 6, 7)
+BACK = (3, 5, 7)
 VIA = (0, 2, 4)
 
 
@@ -129,9 +131,9 @@
         return remote(part, part, *sems, {"tensor": core})
 
     def b_copy(j):
-        third, fourth = xs.at[t, rows(LATE[2]), :], xs.at[t, rows(LATE[3]), :]
-        src = (x.at[rows(LATE[2]), :], swap.at[4], back.at[1], third)[j]
-        dst = (back.at[0], back.at[1], third, fourth)[j]
+        lands = [xs.at[t, rows(c), :] for c in BACK]
+        src = (x.at[rows(BACK[0]), :], swap.at[4], swap.at[5], *lands[:2])[j]
+        dst = (back.at[0], back.at[1], *lands)[j]
         return remote(src, dst, x_send.at[5, j], x_recv.at[5, j], {"section": up})
 
     def x_own(c):
@@ -145,7 +147,6 @@
 
     def x_swap(c):
         k = LATE.index(c)
-        loads[k].wait()
         swap[k] = jnp.where(source, early[k], xs[t, rows(c), :])
 
     def x_swap_send(c):
@@ -166,9 +167,8 @@
     def b_send(j):
         b_copy(j).start()
 
-    def b_choose(_):
-        loads[4].wait()
-        swap[4] = jnp.where(source, early[4], back[0])
+    def b_choose(j):
+        swap[4 + j] = jnp.where(source, early[4 - j], back[j])
 
     def c_copy(c, kind):
         sems = c_send.at[kind, c], c_recv.at[kind, c]
@@ -261,44 +261,54 @@
         row = (c * CHUNK + lax.broadcasted_iota(jnp.int32, (CHUNK, 1), 0)).astype(jnp.float32)
         first = jnp.max(jnp.where(where < row, ends[...], 0.0), axis=1, keepdims=True)
 
-        def score(j, diagonal):
-            col = (j * CHUNK + lax.broadcasted_iota(jnp.int32, (1, CHUNK), 1)).astype(jnp.float32)
+        def keys(p):
+            return pl.ds(pl.multiple_of(p * WIDE, WIDE), WIDE)
+
+        def folded(values, join):
+            parts = [values[:, k * HD : (k + 1) * HD] for k in range(WIDE // HD)]
+            while len(parts) > 1:
+                parts = [join(parts[k], parts[k + 1]) for k in range(0, len(parts), 2)]
+            return parts[0]
+
+        def score(p, diagonal):
+            col = (p * WIDE + lax.broadcasted_iota(jnp.int32, (1, WIDE), 1)).astype(jnp.float32)
             allowed = col >= first
             if diagonal:
                 allowed = allowed & (col <= row)
             for h in range(2):
                 lanes = slice(h * HD, (h + 1) * HD)
                 scores = lax.dot_general(
-                    qb[:, lanes], kb[rows(j), lanes], (((1,), (1,)), ((), ())),
+                    qb[:, lanes], kb[keys(p), lanes], (((1,), (1,)), ((), ())),
                     preferred_element_type=jnp.float32,
                 )
                 scores = jnp.where(allowed, scores, FILL)
-                sb[h, j] = scores
-                top = jnp.maximum(scores[:, :HD], scores[:, HD:])
+                sb[h, p] = scores
+                top = folded(scores, jnp.maximum)
                 tops[h] = top if diagonal else jnp.maximum(tops[h], top)
 
-        def mix(j, highest, last):
+        def mix(p, highest, last):
             for h in range(2):
                 lanes = slice(h * HD, (h + 1) * HD)
-                weights = jnp.exp2((sb[h, j] - highest[h]) * SCALE_LOG2)
-                total = weights[:, :HD] + weights[:, HD:]
+                weights = jnp.exp2((sb[h, p] - highest[h]) * SCALE_LOG2)
+                total = folded(weights, jnp.add)
                 acc = jnp.dot(
-                    weights.astype(jnp.bfloat16), vb[rows(j), lanes], preferred_element_type=jnp.float32
+                    weights.astype(jnp.bfloat16), vb[keys(p), lanes], preferred_element_type=jnp.float32
                 )
                 if last:
                     total = jnp.sum(total + sums[h], axis=1, keepdims=True)
-                    ctx_full[t, rows(j), lanes] = ((acc + accs[h]) / total).astype(jnp.bfloat16)
+                    ctx_full[t, rows(c), lanes] = ((acc + accs[h]) / total).astype(jnp.bfloat16)
                 else:
                     sums[h] += total
                     accs[h] += acc
 
-        score(c, True)
-        lax.fori_loop(0, c, lambda j, _: (score(j, False), 0)[1], 0)
+        whole = c // (WIDE // CHUNK)
+        score(whole, True)
+        lax.fori_loop(0, whole, lambda p, _: (score(p, False), 0)[1], 0)
         highest = [jnp.max(tops[h], axis=1, keepdims=True) for h in range(2)]
         sums[...] = jnp.zeros_like(sums)
         accs[...] = jnp.zeros_like(accs)
-        lax.fori_loop(0, c, lambda j, _: (mix(j, highest, False), 0)[1], 0)
-        mix(c, highest, True)
+        lax.fori_loop(0, whole, lambda p, _: (mix(p, highest, False), 0)[1], 0)
+        mix(whole, highest, True)
         return 0
 
     before = {
@@ -308,16 +318,16 @@
         ],
         1: [
             (w_twin, 0), (w_on, 0), (x_wait, 1), (x_swap, 1), (x_share, 1),
-            (b_wait, 1), (b_send, 2), (x_swap_send, 1),
-        ],
-        2: [(x_swapped, 0), (x_own, 6), (w_twin, 1), (w_on, 1), (x_wait, 2), (x_share, 2)],
+            (b_wait, 1), (b_choose, 1), (x_swap_send, 1), (b_send, 2),
+        ],
+        2: [(x_swapped, 0), (x_own, 6), (w_twin_on, 0), (w_twin, 1), (w_on, 1), (x_wait, 2), (x_share, 2)],
         3: [
-            (b_wait, 2), (b_send, 3), (x_swap, 3), (x_share, 3), (w_twin_on, 0),
+            (b_wait, 2), (b_send, 3), (x_swap, 3), (x_share, 3),
             (x_swap_send, 3), (w_own, 2), (w_own, 3),
         ],
-        4: [(x_swapped, 1), (x_own, 7), (x_wait, 4), (x_share, 4), (w_twin_on, 1)],
+        4: [(x_swapped, 1), (x_wait, 4), (x_share, 4), (w_twin_on, 1)],
         5: [
-            (b_wait, 3), (x_swap, 5), (x_share, 5), (w_own, 4), (x_swap_send, 5), (w_own, 5), (w_whole, 0),
+            (b_wait, 3), (b_send, 4), (x_swap, 5), (x_share, 5), (w_own, 4), (x_swap_send, 5), (w_own, 5), (w_whole, 0),
         ],
         6: [
             (x_swapped, 3), (x_other, 2), (c_done, 0), (c_done, 1), (x_wait, 6), (x_share, 6),
@@ -325,7 +335,7 @@
         ],
         7: [
             (x_swapped, 5), (x_other, 4), (c_swap, 0), (c_done, 2), (c_done, 3), (c_swap_send, 0),
-            (o_first, 0), (w_on, 3), (w_twin, 3), (w_on, 4), (w_twin, 4), (x_wait, 7), (x_share, 7),
+            (o_first, 0), (w_on, 3), (w_twin, 3), (w_on, 4), (w_twin, 4), (b_wait, 4), (x_share, 7),
         ],
         8: [
             (x_other, 6), (c_swap, 2), (o_swap, 0), (c_done, 4), (c_done, 5), (c_swap_send, 2), (o_swap_send, 0),
@@ -352,6 +362,10 @@
     for c in (0, 1, 2, 4):
         x_own(c)
     rounded(3, 8)
+    for load in loads:
+        load.wait()
+    kb[...] = jnp.zeros_like(kb)
+    vb[...] = jnp.zeros_like(vb)
 
     def loop(i, _):
         run(i, before)
@@ -384,8 +398,9 @@
         return 0
 
     lax.fori_loop(0, STEPS, finish, 0)
-    for c in EARLY + LATE[:2]:
+    for c in EARLY[:3] + LATE[:2]:
         x_copy(c, 0).wait_send()
+    b_copy(4).wait_send()
     for k in range(4):
         x_copy(LATE[k], 1).wait_send()
         x_copy(EARLY[k], 4).wait_send()
@@ -454,7 +469,7 @@
         scratch_shapes=[
             pltpu.VMEM((4, ROWS, FEATS), bf16),
             pltpu.VMEM((5, CHUNK, FEATS), bf16),
-            pltpu.VMEM((5, CHUNK, FEATS), bf16),
+            pltpu.VMEM((6, CHUNK, FEATS), bf16),
             pltpu.VMEM((2, CHUNK, FEATS), bf16),
             pltpu.VMEM((3, CHUNK, SHARD), bf16),
             pltpu.VMEM((3, CHUNK, SHARD), bf16),
@@ -465,7 +480,7 @@
             pltpu.VMEM((ROWS, SHARD), bf16),
             pltpu.VMEM((ROWS, SHARD), bf16),
             pltpu.VMEM((1, ROWS), jnp.float32),
-            pltpu.VMEM((2, STEPS, CHUNK, CHUNK), jnp.float32),
+            pltpu.VMEM((2, ROWS // WIDE, CHUNK, WIDE), jnp.float32),
             pltpu.VMEM((2, CHUNK, HD), jnp.float32),
             pltpu.VMEM((2, CHUNK, HD), jnp.float32),
             pltpu.VMEM((2, CHUNK, HD), jnp.float32),

time: 99.7 us -> 98.5 us (0.988)
  Pallas kernels: 98.2 us -> 97 us
    pallas_call x1, Pallas kernels: 91.4 us -> 90.2 us  [shards(): pl.pallas_call(gather_attend, out_shape=(pltpu.VMEM((8, ROWS, SHARD), bf1...]
where the time goes in v5:
time: 98.5 us; the launch traced here: 98.3 us
  Pallas kernels  97 us (98%)
  between operations  1.3 us (1%)
    pallas_call x1, Pallas kernels, shards(): pl.pallas_call(gather_attend, out_shape=(pltpu.VMEM((8, ROWS, SHARD), bf1...  90.2 us
    pallas_call x1, Pallas kernels, shards(): pl.pallas_call(place_blocks, out_shape=(wide,) * 8 + (jax.ShapeDtypeStruc...  6.79 us

profile of v5, /device:TPU:1, one launch (start us, length us, event | category | flops | bytes accessed | tf_op | source)
XLA Modules:
  0.0 98.3 jit_solution(14445980277693210634)
XLA Ops:
  1.3 90.2 %shard_map.178 = (bf16[8,2048,256]{2,1,0:T(8,128)(2,1)S(1)}, bf16[4,2048,256]{2,1,0:T(8,128)(2,1)S(1)}, bf16[4,512,256]{2,1,0:T(8,128)(2,1)S(1)}) custom-call(s32[1]{0:T(128)S(6)} %copy.20.failed, s32[1,2048]{1,0:T(1,128)} %tok.1, bf16[2048,512]{1,0:T(8,128)(2,1)} %bitcast.9, f32[256,256]{1,0:T(8,128)} %bitcast.10, f32[256,256]{1,0:T(8,128)} %bitcast.11, ...), custom_call_target="tpu_custom_call" | custom-call | tf_op jit(solution)/shard_map/pallas_call | solution.py:460
  91.5 6.8 %shard_map.179 = (f32[1,1,2048,256]{3,2,1,0:T(8,128)}, f32[1,1,2048,256]{3,2,1,0:T(8,128)}, f32[1,1,2048,256]{3,2,1,0:T(8,128)}, f32[1,1,2048,256]{3,2,1,0:T(8,1...) custom-call(s32[1]{0:T(128)S(6)} %copy.20.failed, ...), custom_call_target="tpu_custom_call" | custom-call | tf_op jit(solution)/shard_map/pallas_call | solution.py:507

commit v6 on v5

--- a/solution.py
+++ b/solution.py
@@ -338,8 +338,8 @@
             (o_first, 0), (w_on, 3), (w_twin, 3), (w_on, 4), (w_twin, 4), (b_wait, 4), (x_share, 7),
         ],
         8: [
-            (x_other, 6), (c_swap, 2), (o_swap, 0), (c_done, 4), (c_done, 5), (c_swap_send, 2), (o_swap_send, 0),
-            (c_swapped, 0), (w_on, 5), (w_twin, 5), (w_twin_on, 2),
+            (x_other, 6), (c_swap, 2), (c_done, 4), (c_done, 5), (c_swap_send, 2), (o_swap, 0),
+            (w_on, 5), (o_swap_send, 0), (w_twin, 5), (w_twin_on, 2), (c_swapped, 0),
         ],
         9: [
             (x_other, 7), (c_swap, 4), (c_done, 6), (c_swap_send, 4), (c_swapped, 2), (o_swapped, 0),

time: 98.5 us -> 95.6 us (0.971)
  Pallas kernels: 97 us -> 94.2 us
    pallas_call x1, Pallas kernels: 90.2 us -> 87.4 us  [shards(): pl.pallas_call(gather_attend, out_shape=(pltpu.VMEM((8, ROWS, SHARD), bf1...]
where the time goes in v6:
time: 95.6 us; the launch traced here: 95.5 us
  Pallas kernels  94.2 us (99%)
  between operations  1.3 us (1%)
    pallas_call x1, Pallas kernels, shards(): pl.pallas_call(gather_attend, out_shape=(pltpu.VMEM((8, ROWS, SHARD), bf1...  87.4 us
    pallas_call x1, Pallas kernels, shards(): pl.pallas_call(place_blocks, out_shape=(wide,) * 8 + (jax.ShapeDtypeStruc...  6.79 us

profile of v6, /device:TPU:1, one launch (start us, length us, event | category | flops | bytes accessed | tf_op | source)
XLA Modules:
  0.0 95.5 jit_solution(16564023729894469718)
XLA Ops:
  1.3 87.4 %shard_map.178 = (bf16[8,2048,256]{2,1,0:T(8,128)(2,1)S(1)}, bf16[4,2048,256]{2,1,0:T(8,128)(2,1)S(1)}, bf16[4,512,256]{2,1,0:T(8,128)(2,1)S(1)}) custom-call(s32[1]{0:T(128)S(6)} %copy.20.failed, s32[1,2048]{1,0:T(1,128)} %tok.1, bf16[2048,512]{1,0:T(8,128)(2,1)} %bitcast.9, f32[256,256]{1,0:T(8,128)} %bitcast.10, f32[256,256]{1,0:T(8,128)} %bitcast.11, ...), custom_call_target="tpu_custom_call" | custom-call | tf_op jit(solution)/shard_map/pallas_call | solution.py:460
  88.7 6.8 %shard_map.179 = (f32[1,1,2048,256]{3,2,1,0:T(8,128)}, f32[1,1,2048,256]{3,2,1,0:T(8,128)}, f32[1,1,2048,256]{3,2,1,0:T(8,128)}, f32[1,1,2048,256]{3,2,1,0:T(8,1...) custom-call(s32[1]{0:T(128)S(6)} %copy.20.failed, ...), custom_call_target="tpu_custom_call" | custom-call | tf_op jit(solution)/shard_map/pallas_call | solution.py:507
